TPU v7x, 128 devices: a whole 4x4x4 slice. The times are simulated.
128 devices in a mesh: gx: 4 (over y), gy: 16 (over x_lo, z, core), gz: 2 (over x_hi).
Axes of the slice: x: 4 (x_hi: 2, x_lo: 2; x = x_hi * 2 + x_lo), y: 4, z: 4, core: 2. Of those that a mesh axis runs over, the one named last changes fastest.
Arguments:
- heat_source: float32 [64, 512, 2048], P('gz', 'gx', 'gy'), may hold values from -18 to 18
- conductance: float32 [64, 512, 2048], P('gz', 'gx', 'gy'), may hold values from 0.5 to 4
- projection: float32 [2, 4, 16, 3, 128, 128], P('gz', 'gx', 'gy'), may hold values from -1 to 2, as said below
- segment_map: int32 [2, 4, 16, 3, 128], P('gz', 'gx', 'gy'), may hold values from 0 to 127, each once within a row
Outputs:
- thermal_state: float32 [64, 512, 2048], P('gz', 'gx', 'gy')
- multiplier_x: float32 [2, 4, 16, 32, 128], P('gz', 'gx', 'gy')
- multiplier_y: float32 [2, 4, 16, 32, 128], P('gz', 'gx', 'gy')
- multiplier_z: float32 [2, 4, 16, 128, 128], P('gz', 'gx', 'gy')
Inputs may be any that keep to these rules, and one draw needn't show every extreme that they name: projection entries are finite.
All inputs are finite; a program needn't handle non-finite values.
Results may differ from a plain program's by a relative error of at most 0.0001.
Values sent between devices are 32-bit elements; how exact they have to be, the bound alone decides.
No kernel may reach another device: no remote copies, remote signals or barrier semaphores. Data moves between devices by JAX's collectives and lax.ppermute only.
A program may use at most 128 MiB of HBM per device.

v0:
```python
import functools

import jax
import jax.numpy as jnp
from jax import lax
from jax.experimental import pallas as pl
from jax.experimental.pallas import tpu as pltpu
from jax.sharding import PartitionSpec as P

DAMPING_WEIGHT = 0.8
EPSILON = 1e-06
AXES = ("gx", "gy", "gz")
CZ = 32
C = 128
F32 = jnp.float32
UNROLL = 4
WIDE = 16
DEPTH = 8
PARTS = CZ // DEPTH
KEPT = 1.0 - DAMPING_WEIGHT

VM = pl.BlockSpec(memory_space=pltpu.MemorySpace.VMEM)
AWAY = pl.BlockSpec(memory_space=pltpu.MemorySpace.HBM)
BF16 = jnp.bfloat16
PAD = 8


def parts_of(a):
    first = a.astype(BF16)
    rest = a - first.astype(F32)
    second = rest.astype(BF16)
    third = (rest - second.astype(F32)).astype(BF16)
    return first, second, third


def dot(a, parts, d):
    n = a.shape[0]
    mul = functools.partial(jnp.dot, preferred_element_type=F32)
    a1, a2, a3 = parts_of(a)
    r = mul(jnp.concatenate([a1, a2, a3], axis=0), parts[d, :, 0 : 2 * C])
    t = mul(a1, parts[d, :, 2 * C :])
    small = r[2 * n :, :C] + r[n : 2 * n, C:] + t
    return r[:n, :C] + (r[n : 2 * n, :C] + r[:n, C:] + small)


def store_parts(ref, d, a):
    for i, p in enumerate(parts_of(a)):
        ref[d, :, i * C : (i + 1) * C] = p


def lane_of(shape):
    return lax.broadcasted_iota(jnp.int32, shape, len(shape) - 1)


def row_of(shape):
    return lax.broadcasted_iota(jnp.int32, shape, len(shape) - 2)


INNER = slice(PAD, PAD + C)


def zero_ends(ref):
    ref[0] = jnp.zeros((C + 2 * PAD, C), F32)
    ref[CZ + 1] = jnp.zeros((C + 2 * PAD, C), F32)
    for z in range(1, CZ + 1):
        ref[z, 0:PAD, :] = jnp.zeros((PAD, C), F32)
        ref[z, PAD + C :, :] = jnp.zeros((PAD, C), F32)


def in_plane(centre):
    shape = centre.shape
    rows = row_of(shape)
    lanes = lane_of(shape)
    near = jnp.where(rows == 0, 0.0, pltpu.roll(centre, 1, 0))
    near = near + jnp.where(rows == shape[0] - 1, 0.0, pltpu.roll(centre, shape[0] - 1, 0))
    near = near + jnp.where(lanes == 0, 0.0, pltpu.roll(centre, 1, 1))
    return near + jnp.where(lanes == C - 1, 0.0, pltpu.roll(centre, C - 1, 1))


def sweep_planes(src, dst, weight, supply, z, depth, block):
    lanes = lane_of((block, C))
    low = lanes == 0
    high = lanes == C - 1
    for x in range(0, C, block):
        r = PAD + x
        column = [src[z + j, r : r + block, :] for j in range(depth + 2)]
        for j in range(depth):
            centre = column[j + 1]
            near = column[j] + column[j + 2]
            near = near + src[z + j + 1, r - 1 : r - 1 + block, :] + src[z + j + 1, r + 1 : r + 1 + block, :]
            near = near + jnp.where(low, 0.0, pltpu.roll(centre, 1, 1)) + jnp.where(high, 0.0, pltpu.roll(centre, C - 1, 1))
            dst[z + j + 1, r : r + block, :] = KEPT * centre + weight[z + j, x : x + block, :] * (supply[z + j, x : x + block, :] + near)


def sweep(src, dst, weight, supply):
    def planes(i, carry):
        sweep_planes(src, dst, weight, supply, i * WIDE, WIDE, 8)
        return carry

    lax.fori_loop(0, CZ // WIDE, planes, 0)


def row_layer(src, base, at, out):
    for z in range(CZ):
        out[z : z + 1, :] = src[z + base, PAD * base + at : PAD * base + at + 1, :]


def column_layers(src, base, turn):
    group = lane_of((C, C)) // 4

    def plane(z, packed):
        return jnp.where(group == z, pltpu.roll(src[z + base, PAD * base : PAD * base + C, :], 4 * z + 2, 1), packed)

    packed = lax.fori_loop(0, CZ, plane, jnp.zeros((C, C), F32), unroll=CZ)
    turn[...] = packed.T


def layer_rows(i):
    return pl.ds(i, CZ, stride=4)


def pack_columns(turn, low, high):
    turn[...] = jnp.zeros((C, C), F32)
    turn[layer_rows(1), :] = high
    turn[layer_rows(2), :] = low
    return turn[...].T


def column_plane(packed, z):
    lanes = lane_of((C, C))
    edge = (lanes == 0) | (lanes == C - 1)
    return jnp.where(edge, pltpu.roll(packed, C - 2 - 4 * z, 1), 0.0)


def add_rows(dst, faces, sign):
    for z in range(CZ):
        dst[z, 0:1, :] = dst[z, 0:1, :] + sign * faces[0][z : z + 1, :]
        dst[z, C - 1 : C, :] = dst[z, C - 1 : C, :] + sign * faces[1][z : z + 1, :]
    dst[0] = dst[0] + sign * faces[4][...]
    dst[CZ - 1] = dst[CZ - 1] + sign * faces[5][...]


EDGES = (0, 1, C - 2, C - 1)


def rim(low, high, at):
    lanes = lane_of(low.shape)
    a = low if at == 0 else pltpu.roll(low, C - at, 1)
    b = high if at == C - 1 else pltpu.roll(high, C - 1 - at, 1)
    return jnp.where(lanes == 0, a, jnp.where(lanes == C - 1, b, 0.0))


def ends(low, high):
    rows = row_of((CZ, C))
    return jnp.where(rows == 0, low, jnp.where(rows == CZ - 1, high, 0.0))


def lift_layers(faces, turn, inner):
    bx, hx, by, hy, bz, hz = [f[...] for f in faces]
    lanes = lane_of((C, C))
    columns = jnp.where(lanes < 4, pltpu.roll(bz, 2, 1), pltpu.roll(hz, 6, 1)).T
    at = lambda i: columns[i : i + 1, :]
    column = {C - 2: (at(0), at(4)), C - 1: (at(1), at(5)), 0: (at(2), at(6)), 1: (at(3), at(7))}
    edges = EDGES if inner else (0, C - 1)
    on_x = {}
    on_y = {}
    for e in edges:
        on_x[e] = rim(by, hy, e) + ends(bz[e : e + 1, :], hz[e : e + 1, :])
        on_y[e] = rim(bx, hx, e) + ends(*column[e])
    on_x[0] = on_x[0] + bx
    on_x[C - 1] = on_x[C - 1] + hx
    on_y[0] = on_y[0] + by
    on_y[C - 1] = on_y[C - 1] + hy
    packed = pack_columns(turn, by, hy)
    rows = row_of((C, C))
    on_z = {}
    for z in (0, 1, CZ - 2, CZ - 1) if inner else (0, CZ - 1):
        p = column_plane(packed, z)
        p = p + jnp.where(rows == 0, bx[z : z + 1, :], jnp.where(rows == C - 1, hx[z : z + 1, :], 0.0))
        on_z[z] = p + bz if z == 0 else p + hz if z == CZ - 1 else p
    return on_x, on_y, on_z


def layer_weights(weight, wx, wy):
    return (
        {e: wx[i] for i, e in enumerate(EDGES)},
        {e: wy[i] for i, e in enumerate(EDGES)},
        {z: weight[z] for z in (0, 1, CZ - 2, CZ - 1)},
    )


def face_response(layers, weights):
    out = []
    for layer, w, last in zip(layers, weights, (C - 1, C - 1, CZ - 1)):
        for face, inside in ((0, 1), (last, last - 1)):
            once = w[face] * layer[face]
            near = in_plane(once) + w[inside] * layer[inside]
            out.append(KEPT * once + w[face] * (layer[face] + near))
    return out


def fold(t):
    return jnp.sum(t.reshape(t.shape[0] // 8, 8, C), axis=0)


def layer_energy(a, b, weights):
    rows = row_of((CZ, C))
    lanes = lane_of((CZ, C))
    inner = (rows > 0) & (rows < CZ - 1)
    both = inner & (lanes > 0) & (lanes < C - 1)
    acc = jnp.zeros((8, C), F32)
    for layers_a, layers_b, w, last, mask in zip(a, b, weights, (C - 1, C - 1, CZ - 1), (inner, both, None)):
        for e in (0, last):
            t = layers_a[e] * layers_b[e] * w[e]
            acc = acc + fold(t if mask is None else jnp.where(mask, t, 0.0))
    return jnp.sum(acc) / DAMPING_WEIGHT


def places():
    x, y, z = (lax.axis_index(a) for a in AXES)
    more = [i < lax.axis_size(a) - 1 for a, i in zip(AXES, (x, y, z))]
    less = [i > 0 for i in (x, y, z)]
    return (x % 2 == 0, y % 2 == 0, z == 0), more, less


def pick(flag, a, b):
    return lax.select(jnp.broadcast_to(flag, a.shape), a, b)


def pack_sends(sends, faces, index):
    (xeven, yeven, zlow), _, _ = places()
    xa, xb, ya, yb, zz = sends
    for even, a, b, lo, hi in ((xeven, xa, xb, faces[0], faces[1]), (yeven, ya, yb, faces[2], faces[3])):
        s = slice(index * CZ, (index + 1) * CZ)
        a[s, :] = pick(even, hi, lo)
        b[s, :] = pick(even, lo, hi)
    zz[index * C : (index + 1) * C, :] = pick(zlow, faces[5], faces[4])


def own_faces(src, own, turn):
    row_layer(src, 1, 0, own[0])
    row_layer(src, 1, C - 1, own[1])
    column_layers(src, 1, turn)
    own[2][...] = turn[layer_rows(2), :]
    own[3][...] = turn[layer_rows(1), :]
    own[4][...] = src[1, INNER, :]
    own[5][...] = src[CZ, INNER, :]


def first_kernel(heat_in, cond_in, proj_in, segs_in, weight, state, parts, heat, wx, wy, *refs):
    own = refs[:6]
    sends = refs[6:11]
    cond, proj, segs, start, turn, pack, sems, small = refs[11:]
    tables = (pltpu.make_async_copy(proj_in, proj, small.at[0]), pltpu.make_async_copy(segs_in, segs, small.at[1]))

    def copies(i):
        s = pl.ds(i * DEPTH, DEPTH)
        return (
            pltpu.make_async_copy(cond_in.at[s], cond.at[s], sems.at[0, i]),
            pltpu.make_async_copy(heat_in.at[s], heat.at[s], sems.at[1, i]),
        )

    for c in tables:
        c.start()
    for i in range(PARTS):
        for c in copies(i):
            c.start()
    zero_ends(start)
    zero_ends(state)
    pack[...] = jnp.zeros((C, C), F32)
    group = lane_of((C, C)) // 4

    def part(i, carry):
        for c in copies(i):
            c.wait()
        packed = pack[...]
        for j in range(DEPTH):
            z = i * DEPTH + j
            w = DAMPING_WEIGHT / (6.0 + cond[z])
            weight[z] = w
            start[z + 1, INNER, :] = w * heat[z]
            packed = jnp.where(group == z, pltpu.roll(w, 4 * z + 2, 1), packed)
        pack[...] = packed

        @pl.when(i > 0)
        def _():
            sweep_planes(start, state, weight, heat, (i - 1) * DEPTH, DEPTH, 16)

        return carry

    lax.fori_loop(0, PARTS, part, 0)
    sweep_planes(start, state, weight, heat, CZ - DEPTH, DEPTH, 16)
    for c in tables:
        c.wait()
    for d in range(3):
        onehot = jnp.where(row_of((C, C)) == segs[d], 1.0, 0.0).astype(BF16)
        base = sum(lax.dot_general(onehot, p, (((1,), (1,)), ((), ())), preferred_element_type=F32) for p in reversed(parts_of(proj[d])))
        store_parts(parts, d, base)
        for a in (sends[:2], sends[2:4])[d] if d < 2 else ():
            a[CZ : CZ + C, :] = base
        if d == 2:
            sends[4][C : 2 * C, :] = base
    own_faces(state, own, turn)
    pack_sends(sends, [f[...] for f in own], 0)
    for i, e in enumerate(EDGES):
        row_layer(weight, 0, e, wx.at[i])
    turn[...] = pack[...].T
    for i, e in enumerate((2, 3, 0, 1)):
        wy[i] = turn[layer_rows(e), :]


def free_kernel(state, weight, supply, out, *refs):
    own = refs[:6]
    mid, turn = refs[6:]
    zero_ends(mid)
    zero_ends(out)
    sweep(state, mid, weight, supply)
    sweep(mid, out, weight, supply)
    own_faces(out, own, turn)


def jumps(own, got, bases, prev_bases, back_bases, n, lifted):
    (xeven, yeven, zlow), more, less = places()
    xa, xb, ya, yb, zz = got
    for d, (even, a, b, rows) in enumerate(((xeven, xa, xb, n * CZ), (yeven, ya, yb, n * CZ), (zlow, zz, zz, n * C))):
        a = a[0:rows, :]
        b = b[0:rows, :]
        up = own[2 * d + 1][...] - dot(pick(even, a, b), bases, d)
        up = jnp.where(more[d], up, 0.0)
        down = pick(even, b, a) - dot(own[2 * d][...], prev_bases, d)
        back = jnp.where(less[d], -dot(down, back_bases, d), 0.0)
        size = rows // n
        for i in range(n):
            lifted[i][2 * d][...] = back[i * size : (i + 1) * size, :]
            lifted[i][2 * d + 1][...] = up[i * size : (i + 1) * size, :]


def square_sum(a, b):
    return jnp.sum(sum(fold(a[i][...] * b[i][...]) for i in (1, 3, 5)))


def row_of_sums(values):
    lanes = lane_of((1, C))
    row = jnp.zeros((1, C), F32)
    for i, v in enumerate(values):
        row = jnp.where(lanes == i, v, row)
    return row


def second_kernel(first, *refs):
    it = iter(refs)
    take = lambda n: [next(it) for _ in range(n)]
    own = take(6)
    got = take(5)
    (bases,) = take(1)
    prev, back = take(2) if not first else (None, None)
    weight, wx, wy = take(3)
    own_u = take(6)
    lifted = take(6)
    own_uv = take(6)
    sends = take(5)
    if first:
        prev, back = take(2)
    (turn,) = take(1)
    (xeven, yeven, _), _, _ = places()
    if first:
        xa, xb, ya, yb, zz = got
        for d, base in enumerate((pick(xeven, xb[CZ:, :], xa[CZ:, :]), pick(yeven, yb[CZ:, :], ya[CZ:, :]), zz[C:, :])):
            store_parts(prev, d, base)
            store_parts(back, d, base.T)
    jumps(own, got, bases, prev, back, 1, [lifted])
    response = face_response(lift_layers(lifted, turn, True), layer_weights(weight, wx, wy))
    free = [f[...] for f in own_u]
    for o, u, v in zip(own_uv, free, response):
        n = u.shape[0]
        o[0:n, :] = u
        o[n:, :] = v
    pack_sends(sends, free, 0)
    pack_sends(sends, response, 1)


def response_kernel(*refs):
    lifted = refs[:6]
    weight, resp, sums, lift, mid, turn, cols = refs[6:]
    cols[...] = pack_columns(turn, lifted[2][...], lifted[3][...])

    def plane(z, carry):
        lift[z] = column_plane(cols[...], z)
        return carry

    lax.fori_loop(0, CZ, plane, 0, unroll=WIDE)
    add_rows(lift, lifted, 1.0)
    zero_ends(mid)
    zero_ends(resp)

    def scale(z, acc):
        once = weight[z] * lift[z]
        mid[z + 1, INNER, :] = once
        return acc + fold(once * lift[z])

    acc = lax.fori_loop(0, CZ, scale, jnp.zeros((8, C), F32), unroll=UNROLL)
    sweep(mid, resp, weight, lift)
    sums[...] = row_of_sums([square_sum(lifted, lifted), jnp.sum(acc) / DAMPING_WEIGHT])


def merge_sides(low, high):
    return [f for pair in zip(low, high) for f in pair]


def third_kernel(*refs):
    it = iter(refs)
    take = lambda n: [next(it) for _ in range(n)]
    own_uv = take(6)
    got = take(5)
    bases, prev, back, weight, wx, wy, before = take(7)
    high_u, high_v = take(3), take(3)
    (rows,) = take(1)
    low_u, low_v = take(3), take(3)
    (turn,) = take(1)
    lift_u = merge_sides(low_u, high_u)
    lift_v = merge_sides(low_v, high_v)
    jumps(own_uv, got, bases, prev, back, 2, [lift_u, lift_v])
    weights = layer_weights(weight, wx, wy)
    u = lift_layers(lift_u, turn.at[0], False)
    v = lift_layers(lift_v, turn.at[1], False)
    sums = [square_sum(lift_u, lift_u), square_sum(lift_u, lift_v), square_sum(lift_v, lift_v)]
    sums += [layer_energy(u, u, weights), layer_energy(u, v, weights), layer_energy(v, v, weights)]
    lanes = lane_of((1, C))
    row = row_of_sums([0.0, 0.0] + sums)
    row = jnp.where(lanes < 2, before[...], row)
    rows[...] = jnp.broadcast_to(row, (C, C))


def steps(totals):
    row = jnp.sum(totals[...], axis=0, keepdims=True)
    lanes = lane_of((1, C))
    gg, gh, guu, guv, gvv, huu, huv, hvv = [jnp.sum(jnp.where(lanes == i, row, 0.0), axis=1, keepdims=True) for i in range(8)]
    one = gg / (gh + EPSILON)
    two = (guu - 2.0 * one * guv + one * one * gvv) / (huu - 2.0 * one * huv + one * one * hvv + EPSILON)
    return one, two


def fourth_kernel(*refs):
    it = iter(refs)
    take = lambda n: [next(it) for _ in range(n)]
    totals, heat, weight, free, resp = take(5)
    lift_1 = take(6)
    lift_u = take(6)
    lift_v = take(6)
    supply, state = take(2)
    high = take(3)
    own = take(6)
    sends = take(5)
    low = take(3)
    mid, turn, cols = take(3)
    held = merge_sides(low, high)
    one, two = steps(totals)
    for i in range(6):
        held[i][...] = one * lift_1[i][...] + two * (lift_u[i][...] - one * lift_v[i][...])
    cols[...] = pack_columns(turn, held[2][...], held[3][...])
    zero_ends(mid)
    zero_ends(state)

    def plane(z, carry):
        supply[z] = heat[z] - column_plane(cols[...], z)
        state[z + 1, INNER, :] = free[z + 1, INNER, :] - one * resp[z + 1, INNER, :]
        return carry

    lax.fori_loop(0, CZ, plane, 0, unroll=WIDE)
    add_rows(supply, held, -1.0)
    sweep(state, mid, weight, supply)
    sweep(mid, state, weight, supply)
    own_faces(state, own, turn)
    pack_sends(sends, [f[...] for f in own], 0)


def last_kernel(*refs):
    it = iter(refs)
    take = lambda n: [next(it) for _ in range(n)]
    totals, free, resp = take(3)
    held = take(3)
    lift_3 = take(3)
    lift_u = take(3)
    lift_v = take(3)
    (out,) = take(1)
    outs = take(3)
    state, sems = take(2)
    one, two = steps(totals)

    def plane(z, carry):
        state[z] = free[z + 1, INNER, :] - one * resp[z + 1, INNER, :]
        return carry

    copies = []
    for i in range(PARTS):
        lax.fori_loop(i * DEPTH, (i + 1) * DEPTH, plane, 0, unroll=UNROLL)
        s = pl.ds(i * DEPTH, DEPTH)
        copies.append(pltpu.make_async_copy(state.at[s], out.at[s], sems.at[i]))
        copies[-1].start()
    for i in range(3):
        outs[i][...] = held[i][...] + one * lift_3[i][...] + two * (lift_u[i][...] - one * lift_v[i][...])
    for c in copies:
        c.wait()


FIELD = jax.ShapeDtypeStruct((CZ, C, C), F32)
PADDED = jax.ShapeDtypeStruct((CZ + 2, C + 2 * PAD, C), F32)
FACE = jax.ShapeDtypeStruct((CZ, C), F32)
SQUARE = jax.ShapeDtypeStruct((C, C), F32)
FACES = [FACE] * 4 + [SQUARE] * 2
LAYERS = jax.ShapeDtypeStruct((4, CZ, C), F32)
ROW = jax.ShapeDtypeStruct((1, C), F32)
SIDE = [FACE, FACE, SQUARE]
S_SIDE = [pltpu.VMEM(f.shape, F32) for f in SIDE]
S_FIELD = pltpu.VMEM((CZ, C, C), F32)
S_PADDED = pltpu.VMEM((CZ + 2, C + 2 * PAD, C), F32)
PIECES = jax.ShapeDtypeStruct((3, C, 3 * C), BF16)
S_SQUARE = pltpu.VMEM((C, C), F32)


def sends_of(n, extra):
    small = jax.ShapeDtypeStruct((n * CZ + extra, C), F32)
    return [small] * 4 + [jax.ShapeDtypeStruct((n * C + extra, C), F32)]


def call(kernel, outs, scratch, args, us, in_specs=None, out_specs=None):
    return list(
        pl.pallas_call(
            kernel,
            out_shape=tuple(outs),
            in_specs=in_specs or [VM] * len(args),
            out_specs=tuple(out_specs or [VM] * len(outs)),
            scratch_shapes=scratch,
            compiler_params=pltpu.CompilerParams(vmem_limit_bytes=20 * 1024 * 1024),
            cost_estimate=pl.CostEstimate(flops=us * 10**7, transcendentals=0, bytes_accessed=2**20),
        )(*args)
    )


def swap_pairs(along, start):
    nx, ny = lax.axis_size("gx"), lax.axis_size("gy")
    place = lambda x, y: x * ny + y
    pairs = []
    for x in range(nx):
        for y in range(ny):
            i, n = (x, nx) if along == "x" else (y, ny)
            j = i + 1 if i % 2 == start else i - 1
            if 0 <= j < n:
                other = place(j, y) if along == "x" else place(x, j)
            else:
                other = place(x, y ^ 1) if along == "x" else place(x ^ 1, y)
            pairs.append((place(x, y), other))
    return pairs


def exchange(sends):
    xa, xb, ya, yb, zz = sends
    both = ("gx", "gy")
    xa = lax.ppermute(xa, both, swap_pairs("x", 0))
    yb = lax.ppermute(yb, both, swap_pairs("y", 1))
    zz = lax.ppermute(zz, "gz", [(0, 1), (1, 0)])
    xb = lax.ppermute(xb, both, swap_pairs("x", 1))
    ya = lax.ppermute(ya, both, swap_pairs("y", 0))
    return [xa, xb, ya, yb, zz]


def gather_rows(rows):
    rows = lax.all_to_all(rows.reshape(C, 1, C), AXES, 0, 0)
    return rows.reshape(C, C)


def body(heat, cond, projection, segment_map):
    proj = projection[0, 0, 0]
    segs = segment_map.reshape(3, 1, C)
    dma = pltpu.SemaphoreType.DMA
    scratch = [S_FIELD, pltpu.VMEM(proj.shape, F32), pltpu.VMEM(segs.shape, jnp.int32), S_PADDED, S_SQUARE, S_SQUARE, dma((2, PARTS)), dma((2,))]
    outs = [FIELD, PADDED, PIECES, FIELD, LAYERS, LAYERS] + FACES + sends_of(1, C)
    out = call(first_kernel, outs, scratch, [pltpu.with_memory_space_constraint(a, pltpu.MemorySpace.HBM) for a in (heat, cond, proj, segs)], 4, [AWAY] * 4)
    weight, state, bases, heat, wx, wy = out[:6]
    own, sends = out[6:12], out[12:]
    supply = heat
    prev = []
    held = None
    for pair in range(2):
        first = pair == 0
        got = exchange(sends)
        out = call(free_kernel, [PADDED] + FACES, [S_PADDED, S_SQUARE], (state, weight, supply), 3)
        free, own_u = out[0], out[1:]
        args = own + got + [bases] + prev + [weight, wx, wy] + own_u
        stacked = [jax.ShapeDtypeStruct((2 * f.shape[0], C), F32) for f in FACES]
        outs = FACES + stacked + sends_of(2, 0) + ([PIECES, PIECES] if first else [])
        out = call(functools.partial(second_kernel, first), outs, [S_SQUARE], args, 2)
        lift_1, own_uv, sends = out[:6], out[6:12], out[12:17]
        if first:
            prev = out[17:]
        got = exchange(sends)
        resp, sums = call(response_kernel, [PADDED, ROW], [S_FIELD, S_PADDED, S_SQUARE, S_SQUARE], lift_1 + [weight], 3)
        args = own_uv + got + [bases] + prev + [weight, wx, wy, sums]
        outs = SIDE + SIDE + [SQUARE] + (SIDE + SIDE if first else [])
        scratch = ([] if first else S_SIDE + S_SIDE) + [pltpu.VMEM((2, C, C), F32)]
        out = call(third_kernel, outs, scratch, args, 2)
        high_u, high_v, rows = out[:3], out[3:6], out[6]
        totals = gather_rows(rows)
        if first:
            args = [totals, heat, weight, free, resp] + lift_1 + merge_sides(out[7:10], high_u) + merge_sides(out[10:13], high_v)
            outs = [FIELD, PADDED] + SIDE + FACES + sends_of(1, 0)
            out = call(fourth_kernel, outs, S_SIDE + [S_PADDED, S_SQUARE, S_SQUARE], args, 5)
            supply, state, held, own, sends = out[0], out[1], out[2:5], out[5:11], out[11:]
    args = [totals, free, resp] + held + [lift_1[i] for i in (1, 3, 5)] + high_u + high_v
    state, mx, my, mz = call(last_kernel, [FIELD, FACE, FACE, SQUARE], [S_FIELD, dma((PARTS,))], args, 2, None, [AWAY, VM, VM, VM])
    return state, mx[None, None, None], my[None, None, None], mz[None, None, None]


def solution(mesh):
    field = P("gz", "gx", "gy")
    in_specs = (field, field, P("gz", "gx", "gy", None, None, None), P("gz", "gx", "gy", None, None))
    face = P("gz", "gx", "gy", None, None)
    return jax.shard_map(body, mesh=mesh, in_specs=in_specs, out_specs=(field, face, face, face), check_vma=False)
```

profile of v0, /device:TPU:1, one launch (start us, length us, event | category | flops | bytes accessed | tf_op | source)
XLA Modules:
  0.0 88.1 jit_solution(6903213858071802543)
XLA Ops:
  0.6 4.5 %shard_map.75 = (f32[32,128,128]{2,1,0:T(8,128)S(1)}, f32[34,144,128]{2,1,0:T(8,128)S(1)}, bf16[3,128,384]{2,1,0:T(8,128)(2,1)S(1)}, f32[32,128,128]{2,1,0:T(8,1...) custom-call(f32[32,128,128]{2,1,0:T(8,128)} %heat_in.1, ...), custom_call_target="tpu_custom_call" | custom-call | flops 40000000 | bytes 1048576 | tf_op jit(solution)/shard_map/pallas_call | solution.py:528
  5.2 3.6 %collective-permute-start.4 = (f32[256,128]{1,0:T(8,128)S(1)}, f32[256,128]{1,0:T(8,128)S(1)}, u32[]{:S(2)}, u32[]{:S(2)}) collective-permute-start(f32[256,128]{1,0:T(8,128)S(1)} %get-tuple-element.125), channel_id=1, source_target_pairs={{0,1},{1,0},{2,3},{3,2},{4,5},{5,4},{6,7},{7,6},{8,9},{9,8},{10,11... | collective-permute-start | bytes 393224 | tf_op jit(solution)/shard_map/ppermute | solution.py:561
  8.8 1.3 %collective-permute-start = (f32[160,128]{1,0:T(8,128)S(1)}, f32[160,128]{1,0:T(8,128)S(1)}, u32[]{:S(2)}, u32[]{:S(2)}) collective-permute-start(f32[160,128]{1,0:T(8,128)S(1)} %get-tuple-element.121), channel_id=1, source_target_pairs={{0,32},{2,34},{4,36},{6,38},{8,40},{10,42},{12,44},{14,46},{16,48}... | collective-permute-start | bytes 245768 | tf_op jit(solution)/shard_map/ppermute | solution.py:559
  10.1 1.2 %collective-permute-start.1 = (f32[160,128]{1,0:T(8,128)S(1)}, f32[160,128]{1,0:T(8,128)S(1)}, u32[]{:S(2)}, u32[]{:S(2)}) collective-permute-start(f32[160,128]{1,0:T(8,128)S(1)} %get-tuple-element.122), channel_id=1, source_target_pairs={{0,2},{2,0},{4,6},{6,4},{8,10},{10,8},{12,14},{14,12},{16,18},{18,... | collective-permute-start | bytes 245768 | tf_op jit(solution)/shard_map/ppermute | solution.py:562
  11.4 2.0 %collective-permute-start.3 = (f32[160,128]{1,0:T(8,128)S(1)}, f32[160,128]{1,0:T(8,128)S(1)}, u32[]{:S(2)}, u32[]{:S(2)}) collective-permute-start(f32[160,128]{1,0:T(8,128)S(1)} %get-tuple-element.124), channel_id=1, source_target_pairs={{0,32},{2,4},{4,2},{6,8},{8,6},{10,12},{12,10},{14,16},{16,14},{18... | collective-permute-start | bytes 245768 | tf_op jit(solution)/shard_map/ppermute | solution.py:560
  13.4 3.2 %shard_map.76 = (f32[34,144,128]{2,1,0:T(8,128)S(1)}, f32[32,128]{1,0:T(8,128)S(1)}, f32[32,128]{1,0:T(8,128)S(1)}, f32[32,128]{1,0:T(8,128)S(1)}, f32[32,128]{1...) custom-call(f32[34,144,128]{2,1,0:T(8,128)S(1)} %get-tuple-element.130.state, ...), custom_call_target="tpu_custom_call" | custom-call | flops 30000000 | bytes 1048576 | tf_op jit(solution)/shard_map/pallas_call | solution.py:528
  16.6 0.0 collective-permute-done.1.refs_7_
  16.6 0.0 collective-permute-done.3.refs_9_
  16.6 1.2 %shard_map.77 = (f32[32,128]{1,0:T(8,128)S(1)}, f32[32,128]{1,0:T(8,128)S(1)}, f32[32,128]{1,0:T(8,128)S(1)}, f32[32,128]{1,0:T(8,128)S(1)}, f32[128,128]{1,0:T(...) custom-call(f32[32,128]{1,0:T(8,128)S(1)} %get-tuple-element.115.ref, ...), custom_call_target="tpu_custom_call" | custom-call | flops 20000000 | bytes 1048576 | tf_op jit(solution)/shard_map/pallas_call | solution.py:528
  17.8 0.3 collective-permute-start.9
  18.1 2.1 %collective-permute-start.5 = (f32[64,128]{1,0:T(8,128)S(1)}, f32[64,128]{1,0:T(8,128)S(1)}, u32[]{:S(2)}, u32[]{:S(2)}) collective-permute-start(f32[64,128]{1,0:T(8,128)S(1)} %get-tuple-element.144), channel_id=1, source_target_pairs={{0,32},{2,34},{4,36},{6,38},{8,40},{10,42},{12,44},{14,46},{16,48}... | collective-permute-start | bytes 98312 | tf_op jit(solution)/shard_map/ppermute | solution.py:559
  20.2 0.2 collective-permute-start.6
  20.4 0.3 collective-permute-start.7
  20.7 1.5 %collective-permute-start.8 = (f32[64,128]{1,0:T(8,128)S(1)}, f32[64,128]{1,0:T(8,128)S(1)}, u32[]{:S(2)}, u32[]{:S(2)}) collective-permute-start(f32[64,128]{1,0:T(8,128)S(1)} %get-tuple-element.147), channel_id=1, source_target_pairs={{0,32},{2,4},{4,2},{6,8},{8,6},{10,12},{12,10},{14,16},{16,14},{18... | collective-permute-start | bytes 98312 | tf_op jit(solution)/shard_map/ppermute | solution.py:560
  22.3 2.5 %shard_map.78 = (f32[34,144,128]{2,1,0:T(8,128)S(1)}, f32[1,128]{1,0:T(1,128)S(1)}) custom-call(f32[32,128]{1,0:T(8,128)S(1)} %get-tuple-element.151.refs_0_.refs_5_, f32[32,128]{1,0:T(8,128)S(1)} %get-tuple-element.152.refs_1_.refs_6_, f32[32,128]{1,0:T(8,128)S(1)} %get-tuple-element.153.refs_2_.refs_7_, f32[32,128]{1,0:T(8,128)S(1)} %get-tuple-element.154.refs_3_.refs_8_, ...), custom_call_target="tpu_custom_call" | custom-call | flops 30000000 | bytes 1048576 | tf_op jit(solution)/shard_map/pallas_call | solution.py:528
  24.8 1.5 %shard_map.79 = (f32[32,128]{1,0:T(8,128)S(1)}, f32[32,128]{1,0:T(8,128)S(1)}, f32[128,128]{1,0:T(8,128)S(1)}, f32[32,128]{1,0:T(8,128)S(1)}, f32[32,128]{1,0:T(...) custom-call(f32[64,128]{1,0:T(8,128)S(1)} %get-tuple-element.138.ref, ...), custom_call_target="tpu_custom_call" | custom-call | flops 20000000 | bytes 1048576 | tf_op jit(solution)/shard_map/pallas_call | solution.py:528
  26.4 20.6 %all_to_all.10 = f32[128,1,128]{2,1,0:T(1,128)S(1)} all-to-all(f32[128,1,128]{2,1,0:T(1,128)S(1)} %bitcast.15), channel_id=1, replica_groups=mesh['gx'=4,'gy'=16,'gz'=2] {'gx','gy','gz'}, dimensions={0} | all-to-all | bytes 131072 | tf_op jit(solution)/shard_map/all_to_all | solution.py:568
  47.0 4.3 %shard_map.80 = (f32[32,128,128]{2,1,0:T(8,128)S(1)}, f32[34,144,128]{2,1,0:T(8,128)S(1)}, f32[32,128]{1,0:T(8,128)S(1)}, f32[32,128]{1,0:T(8,128)S(1)}, f32[128...) custom-call(f32[128,128]{1,0:T(8,128)S(1)} %bitcast.13, ...), custom_call_target="tpu_custom_call" | custom-call | flops 50000000 | bytes 1048576 | tf_op jit(solution)/shard_map/pallas_call | solution.py:528
  51.3 1.1 %collective-permute-start.14 = (f32[128,128]{1,0:T(8,128)S(1)}, f32[128,128]{1,0:T(8,128)S(1)}, u32[]{:S(2)}, u32[]{:S(2)}) collective-permute-start(f32[128,128]{1,0:T(8,128)S(1)} %get-tuple-element.183), channel_id=1, source_target_pairs={{0,1},{1,0},{2,3},{3,2},{4,5},{5,4},{6,7},{7,6},{8,9},{9,8},{10,11... | collective-permute-start | bytes 196616 | tf_op jit(solution)/shard_map/ppermute | solution.py:561
  52.4 0.4 collective-permute-start.10
  52.8 1.1 %collective-permute-start.11 = (f32[32,128]{1,0:T(8,128)S(1)}, f32[32,128]{1,0:T(8,128)S(1)}, u32[]{:S(2)}, u32[]{:S(2)}) collective-permute-start(f32[32,128]{1,0:T(8,128)S(1)} %get-tuple-element.180), channel_id=1, source_target_pairs={{0,2},{2,0},{4,6},{6,4},{8,10},{10,8},{12,14},{14,12},{16,18},{18,... | collective-permute-start | bytes 49160 | tf_op jit(solution)/shard_map/ppermute | solution.py:562
  53.9 0.9 %collective-permute-start.13 = (f32[32,128]{1,0:T(8,128)S(1)}, f32[32,128]{1,0:T(8,128)S(1)}, u32[]{:S(2)}, u32[]{:S(2)}) collective-permute-start(f32[32,128]{1,0:T(8,128)S(1)} %get-tuple-element.182), channel_id=1, source_target_pairs={{0,32},{2,4},{4,2},{6,8},{8,6},{10,12},{12,10},{14,16},{16,14},{18... | collective-permute-start | bytes 49160 | tf_op jit(solution)/shard_map/ppermute | solution.py:560
  54.8 3.2 %shard_map.81 = (f32[34,144,128]{2,1,0:T(8,128)S(1)}, f32[32,128]{1,0:T(8,128)S(1)}, f32[32,128]{1,0:T(8,128)S(1)}, f32[32,128]{1,0:T(8,128)S(1)}, f32[32,128]{1...) custom-call(f32[34,144,128]{2,1,0:T(8,128)S(1)} %get-tuple-element.184.state, ...), custom_call_target="tpu_custom_call" | custom-call | flops 30000000 | bytes 1048576 | tf_op jit(solution)/shard_map/pallas_call | solution.py:528
  58.0 1.2 %shard_map.82 = (f32[32,128]{1,0:T(8,128)S(1)}, f32[32,128]{1,0:T(8,128)S(1)}, f32[32,128]{1,0:T(8,128)S(1)}, f32[32,128]{1,0:T(8,128)S(1)}, f32[128,128]{1,0:T(...) custom-call(f32[32,128]{1,0:T(8,128)S(1)} %get-tuple-element.173.ref, ...), custom_call_target="tpu_custom_call" | custom-call | flops 20000000 | bytes 1048576 | tf_op jit(solution)/shard_map/pallas_call | solution.py:528
  59.2 1.8 %collective-permute-start.19 = (f32[256,128]{1,0:T(8,128)S(1)}, f32[256,128]{1,0:T(8,128)S(1)}, u32[]{:S(2)}, u32[]{:S(2)}) collective-permute-start(f32[256,128]{1,0:T(8,128)S(1)} %get-tuple-element.202), channel_id=1, source_target_pairs={{0,1},{1,0},{2,3},{3,2},{4,5},{5,4},{6,7},{7,6},{8,9},{9,8},{10,11... | collective-permute-start | bytes 393224 | tf_op jit(solution)/shard_map/ppermute | solution.py:561
  61.0 1.1 %collective-permute-start.15 = (f32[64,128]{1,0:T(8,128)S(1)}, f32[64,128]{1,0:T(8,128)S(1)}, u32[]{:S(2)}, u32[]{:S(2)}) collective-permute-start(f32[64,128]{1,0:T(8,128)S(1)} %get-tuple-element.198), channel_id=1, source_target_pairs={{0,32},{2,34},{4,36},{6,38},{8,40},{10,42},{12,44},{14,46},{16,48}... | collective-permute-start | bytes 98312 | tf_op jit(solution)/shard_map/ppermute | solution.py:559
  62.1 1.0 %collective-permute-start.16 = (f32[64,128]{1,0:T(8,128)S(1)}, f32[64,128]{1,0:T(8,128)S(1)}, u32[]{:S(2)}, u32[]{:S(2)}) collective-permute-start(f32[64,128]{1,0:T(8,128)S(1)} %get-tuple-element.199), channel_id=1, source_target_pairs={{0,2},{2,0},{4,6},{6,4},{8,10},{10,8},{12,14},{14,12},{16,18},{18,... | collective-permute-start | bytes 98312 | tf_op jit(solution)/shard_map/ppermute | solution.py:562
  63.1 1.6 %collective-permute-start.18 = (f32[64,128]{1,0:T(8,128)S(1)}, f32[64,128]{1,0:T(8,128)S(1)}, u32[]{:S(2)}, u32[]{:S(2)}) collective-permute-start(f32[64,128]{1,0:T(8,128)S(1)} %get-tuple-element.201), channel_id=1, source_target_pairs={{0,32},{2,4},{4,2},{6,8},{8,6},{10,12},{12,10},{14,16},{16,14},{18... | collective-permute-start | bytes 98312 | tf_op jit(solution)/shard_map/ppermute | solution.py:560
  64.7 2.5 %shard_map.83 = (f32[34,144,128]{2,1,0:T(8,128)S(1)}, f32[1,128]{1,0:T(1,128)S(1)}) custom-call(f32[32,128]{1,0:T(8,128)S(1)} %get-tuple-element.203.refs_0_, f32[32,128]{1,0:T(8,128)S(1)} %get-tuple-element.204.refs_1_.refs_6_, f32[32,128]{1,0:T(8,128)S(1)} %get-tuple-element.205.refs_2_, f32[32,128]{1,0:T(8,128)S(1)} %get-tuple-element.206.refs_3_.refs_7_, ...), custom_call_target="tpu_custom_call" | custom-call | flops 30000000 | bytes 1048576 | tf_op jit(solution)/shard_map/pallas_call | solution.py:528
  67.2 1.5 %shard_map.84 = (f32[32,128]{1,0:T(8,128)S(1)}, f32[32,128]{1,0:T(8,128)S(1)}, f32[128,128]{1,0:T(8,128)S(1)}, f32[32,128]{1,0:T(8,128)S(1)}, f32[32,128]{1,0:T(...) custom-call(f32[64,128]{1,0:T(8,128)S(1)} %get-tuple-element.192.refs_0_, ...), custom_call_target="tpu_custom_call" | custom-call | flops 20000000 | bytes 1048576 | tf_op jit(solution)/shard_map/pallas_call | solution.py:528
  68.8 17.0 %all_to_all.11 = f32[128,1,128]{2,1,0:T(1,128)S(1)} all-to-all(f32[128,1,128]{2,1,0:T(1,128)S(1)} %bitcast.16), channel_id=1, replica_groups=mesh['gx'=4,'gy'=16,'gz'=2] {'gx','gy','gz'}, dimensions={0} | all-to-all | bytes 131072 | tf_op jit(solution)/shard_map/all_to_all | solution.py:568
  85.8 2.2 %shard_map.85 = (f32[32,128,128]{2,1,0:T(8,128)}, f32[32,128]{1,0:T(8,128)}, f32[32,128]{1,0:T(8,128)}, f32[128,128]{1,0:T(8,128)}) custom-call(f32[128,128]{1,0:T(8,128)S(1)} %bitcast.14, f32[34,144,128]{2,1,0:T(8,128)S(1)} %get-tuple-element.211.refs_1_, f32[34,144,128]{2,1,0:T(8,128)S(1)} %get-tuple-element.212.refs_2_, ...), custom_call_target="tpu_custom_call" | custom-call | flops 20000000 | bytes 1048576 | tf_op jit(solution)/shard_map/pallas_call | solution.py:528
  (21 shorter events, 0.1 us)
Async XLA Ops:
  5.2 11.4 %collective-permute-start.4 = (f32[256,128]{1,0:T(8,128)S(1)}, f32[256,128]{1,0:T(8,128)S(1)}, u32[]{:S(2)}, u32[]{:S(2)}) collective-permute-start(f32[256,128]{1,0:T(8,128)S(1)} %get-tuple-element.125), channel_id=1, source_target_pairs={{0,1},{1,0},{2,3},{3,2},{4,5},{5,4},{6,7},{7,6},{8,9},{9,8},{10,11... | collective-permute-start | bytes 393224 | tf_op jit(solution)/shard_map/ppermute | solution.py:561
  8.8 7.8 %collective-permute-start = (f32[160,128]{1,0:T(8,128)S(1)}, f32[160,128]{1,0:T(8,128)S(1)}, u32[]{:S(2)}, u32[]{:S(2)}) collective-permute-start(f32[160,128]{1,0:T(8,128)S(1)} %get-tuple-element.121), channel_id=1, source_target_pairs={{0,32},{2,34},{4,36},{6,38},{8,40},{10,42},{12,44},{14,46},{16,48}... | collective-permute-start | bytes 245768 | tf_op jit(solution)/shard_map/ppermute | solution.py:559
  10.1 6.5 %collective-permute-start.1 = (f32[160,128]{1,0:T(8,128)S(1)}, f32[160,128]{1,0:T(8,128)S(1)}, u32[]{:S(2)}, u32[]{:S(2)}) collective-permute-start(f32[160,128]{1,0:T(8,128)S(1)} %get-tuple-element.122), channel_id=1, source_target_pairs={{0,2},{2,0},{4,6},{6,4},{8,10},{10,8},{12,14},{14,12},{16,18},{18,... | collective-permute-start | bytes 245768 | tf_op jit(solution)/shard_map/ppermute | solution.py:562
  11.4 5.2 %collective-permute-start.2 = (f32[160,128]{1,0:T(8,128)S(1)}, f32[160,128]{1,0:T(8,128)S(1)}, u32[]{:S(2)}, u32[]{:S(2)}) collective-permute-start(f32[160,128]{1,0:T(8,128)S(1)} %get-tuple-element.123), channel_id=1, source_target_pairs={{0,2},{2,0},{4,6},{6,4},{8,10},{10,8},{12,14},{14,12},{16,18},{18,... | collective-permute-start | bytes 245768 | tf_op jit(solution)/shard_map/ppermute | solution.py:563
  11.4 5.2 %collective-permute-start.3 = (f32[160,128]{1,0:T(8,128)S(1)}, f32[160,128]{1,0:T(8,128)S(1)}, u32[]{:S(2)}, u32[]{:S(2)}) collective-permute-start(f32[160,128]{1,0:T(8,128)S(1)} %get-tuple-element.124), channel_id=1, source_target_pairs={{0,32},{2,4},{4,2},{6,8},{8,6},{10,12},{12,10},{14,16},{16,14},{18... | collective-permute-start | bytes 245768 | tf_op jit(solution)/shard_map/ppermute | solution.py:560
  17.8 7.0 %collective-permute-start.9 = (f32[256,128]{1,0:T(8,128)S(1)}, f32[256,128]{1,0:T(8,128)S(1)}, u32[]{:S(2)}, u32[]{:S(2)}) collective-permute-start(f32[256,128]{1,0:T(8,128)S(1)} %get-tuple-element.148), channel_id=1, source_target_pairs={{0,1},{1,0},{2,3},{3,2},{4,5},{5,4},{6,7},{7,6},{8,9},{9,8},{10,11... | collective-permute-start | bytes 393224 | tf_op jit(solution)/shard_map/ppermute | solution.py:561
  18.1 6.6 %collective-permute-start.5 = (f32[64,128]{1,0:T(8,128)S(1)}, f32[64,128]{1,0:T(8,128)S(1)}, u32[]{:S(2)}, u32[]{:S(2)}) collective-permute-start(f32[64,128]{1,0:T(8,128)S(1)} %get-tuple-element.144), channel_id=1, source_target_pairs={{0,32},{2,34},{4,36},{6,38},{8,40},{10,42},{12,44},{14,46},{16,48}... | collective-permute-start | bytes 98312 | tf_op jit(solution)/shard_map/ppermute | solution.py:559
  20.2 4.6 %collective-permute-start.6 = (f32[64,128]{1,0:T(8,128)S(1)}, f32[64,128]{1,0:T(8,128)S(1)}, u32[]{:S(2)}, u32[]{:S(2)}) collective-permute-start(f32[64,128]{1,0:T(8,128)S(1)} %get-tuple-element.145), channel_id=1, source_target_pairs={{0,2},{2,0},{4,6},{6,4},{8,10},{10,8},{12,14},{14,12},{16,18},{18,... | collective-permute-start | bytes 98312 | tf_op jit(solution)/shard_map/ppermute | solution.py:562
  20.4 4.4 %collective-permute-start.7 = (f32[64,128]{1,0:T(8,128)S(1)}, f32[64,128]{1,0:T(8,128)S(1)}, u32[]{:S(2)}, u32[]{:S(2)}) collective-permute-start(f32[64,128]{1,0:T(8,128)S(1)} %get-tuple-element.146), channel_id=1, source_target_pairs={{0,2},{2,0},{4,6},{6,4},{8,10},{10,8},{12,14},{14,12},{16,18},{18,... | collective-permute-start | bytes 98312 | tf_op jit(solution)/shard_map/ppermute | solution.py:563
  20.7 4.1 %collective-permute-start.8 = (f32[64,128]{1,0:T(8,128)S(1)}, f32[64,128]{1,0:T(8,128)S(1)}, u32[]{:S(2)}, u32[]{:S(2)}) collective-permute-start(f32[64,128]{1,0:T(8,128)S(1)} %get-tuple-element.147), channel_id=1, source_target_pairs={{0,32},{2,4},{4,2},{6,8},{8,6},{10,12},{12,10},{14,16},{16,14},{18... | collective-permute-start | bytes 98312 | tf_op jit(solution)/shard_map/ppermute | solution.py:560
  51.3 6.8 %collective-permute-start.14 = (f32[128,128]{1,0:T(8,128)S(1)}, f32[128,128]{1,0:T(8,128)S(1)}, u32[]{:S(2)}, u32[]{:S(2)}) collective-permute-start(f32[128,128]{1,0:T(8,128)S(1)} %get-tuple-element.183), channel_id=1, source_target_pairs={{0,1},{1,0},{2,3},{3,2},{4,5},{5,4},{6,7},{7,6},{8,9},{9,8},{10,11... | collective-permute-start | bytes 196616 | tf_op jit(solution)/shard_map/ppermute | solution.py:561
  52.4 5.6 %collective-permute-start.10 = (f32[32,128]{1,0:T(8,128)S(1)}, f32[32,128]{1,0:T(8,128)S(1)}, u32[]{:S(2)}, u32[]{:S(2)}) collective-permute-start(f32[32,128]{1,0:T(8,128)S(1)} %get-tuple-element.179), channel_id=1, source_target_pairs={{0,32},{2,34},{4,36},{6,38},{8,40},{10,42},{12,44},{14,46},{16,48}... | collective-permute-start | bytes 49160 | tf_op jit(solution)/shard_map/ppermute | solution.py:559
  52.8 5.2 %collective-permute-start.11 = (f32[32,128]{1,0:T(8,128)S(1)}, f32[32,128]{1,0:T(8,128)S(1)}, u32[]{:S(2)}, u32[]{:S(2)}) collective-permute-start(f32[32,128]{1,0:T(8,128)S(1)} %get-tuple-element.180), channel_id=1, source_target_pairs={{0,2},{2,0},{4,6},{6,4},{8,10},{10,8},{12,14},{14,12},{16,18},{18,... | collective-permute-start | bytes 49160 | tf_op jit(solution)/shard_map/ppermute | solution.py:562
  53.9 4.2 %collective-permute-start.12 = (f32[32,128]{1,0:T(8,128)S(1)}, f32[32,128]{1,0:T(8,128)S(1)}, u32[]{:S(2)}, u32[]{:S(2)}) collective-permute-start(f32[32,128]{1,0:T(8,128)S(1)} %get-tuple-element.181), channel_id=1, source_target_pairs={{0,2},{2,0},{4,6},{6,4},{8,10},{10,8},{12,14},{14,12},{16,18},{18,... | collective-permute-start | bytes 49160 | tf_op jit(solution)/shard_map/ppermute | solution.py:563
  53.9 4.2 %collective-permute-start.13 = (f32[32,128]{1,0:T(8,128)S(1)}, f32[32,128]{1,0:T(8,128)S(1)}, u32[]{:S(2)}, u32[]{:S(2)}) collective-permute-start(f32[32,128]{1,0:T(8,128)S(1)} %get-tuple-element.182), channel_id=1, source_target_pairs={{0,32},{2,4},{4,2},{6,8},{8,6},{10,12},{12,10},{14,16},{16,14},{18... | collective-permute-start | bytes 49160 | tf_op jit(solution)/shard_map/ppermute | solution.py:560
  59.2 8.0 %collective-permute-start.19 = (f32[256,128]{1,0:T(8,128)S(1)}, f32[256,128]{1,0:T(8,128)S(1)}, u32[]{:S(2)}, u32[]{:S(2)}) collective-permute-start(f32[256,128]{1,0:T(8,128)S(1)} %get-tuple-element.202), channel_id=1, source_target_pairs={{0,1},{1,0},{2,3},{3,2},{4,5},{5,4},{6,7},{7,6},{8,9},{9,8},{10,11... | collective-permute-start | bytes 393224 | tf_op jit(solution)/shard_map/ppermute | solution.py:561
  61.0 6.2 %collective-permute-start.15 = (f32[64,128]{1,0:T(8,128)S(1)}, f32[64,128]{1,0:T(8,128)S(1)}, u32[]{:S(2)}, u32[]{:S(2)}) collective-permute-start(f32[64,128]{1,0:T(8,128)S(1)} %get-tuple-element.198), channel_id=1, source_target_pairs={{0,32},{2,34},{4,36},{6,38},{8,40},{10,42},{12,44},{14,46},{16,48}... | collective-permute-start | bytes 98312 | tf_op jit(solution)/shard_map/ppermute | solution.py:559
  62.1 5.1 %collective-permute-start.16 = (f32[64,128]{1,0:T(8,128)S(1)}, f32[64,128]{1,0:T(8,128)S(1)}, u32[]{:S(2)}, u32[]{:S(2)}) collective-permute-start(f32[64,128]{1,0:T(8,128)S(1)} %get-tuple-element.199), channel_id=1, source_target_pairs={{0,2},{2,0},{4,6},{6,4},{8,10},{10,8},{12,14},{14,12},{16,18},{18,... | collective-permute-start | bytes 98312 | tf_op jit(solution)/shard_map/ppermute | solution.py:562
  63.1 4.2 %collective-permute-start.17 = (f32[64,128]{1,0:T(8,128)S(1)}, f32[64,128]{1,0:T(8,128)S(1)}, u32[]{:S(2)}, u32[]{:S(2)}) collective-permute-start(f32[64,128]{1,0:T(8,128)S(1)} %get-tuple-element.200), channel_id=1, source_target_pairs={{0,2},{2,0},{4,6},{6,4},{8,10},{10,8},{12,14},{14,12},{16,18},{18,... | collective-permute-start | bytes 98312 | tf_op jit(solution)/shard_map/ppermute | solution.py:563
  63.1 4.2 %collective-permute-start.18 = (f32[64,128]{1,0:T(8,128)S(1)}, f32[64,128]{1,0:T(8,128)S(1)}, u32[]{:S(2)}, u32[]{:S(2)}) collective-permute-start(f32[64,128]{1,0:T(8,128)S(1)} %get-tuple-element.201), channel_id=1, source_target_pairs={{0,32},{2,4},{4,2},{6,8},{8,6},{10,12},{12,10},{14,16},{16,14},{18... | collective-permute-start | bytes 98312 | tf_op jit(solution)/shard_map/ppermute | solution.py:560
where the time goes:
time: 88.2 us; the launch traced here: 88.1 us
  blocking collectives  37.6 us (43%)
  Pallas kernels  27.8 us (32%)
  starting transfers between devices  21.6 us (24%)
  between operations  1 us (1%)
    all_to_all x2, blocking collectives, gather_rows(): rows = lax.all_to_all(rows.reshape(C, 1, C), AXES, 0, 0)  37.6 us
    pallas_call x11, Pallas kernels, call(): pl.pallas_call(kernel, out_shape=tuple(outs), in_specs=in_specs or [VM] *...  27.8 us
    ppermute x4, starting transfers between devices, exchange(): zz = lax.ppermute(zz, 'gz', [(0, 1), (1, 0)])  6.89 us
    ppermute x4, starting transfers between devices, exchange(): yb = lax.ppermute(yb, both, swap_pairs('y', 1))  6.11 us
    ppermute x4, starting transfers between devices, exchange(): xa = lax.ppermute(xa, both, swap_pairs('x', 0))  4.82 us
    ppermute x4, starting transfers between devices, exchange(): xb = lax.ppermute(xb, both, swap_pairs('x', 1))  3.51 us
  transfers between devices with their start and end apart: 20, of which 0 were waited for; matrix products, arithmetic and copies ran while one was open for 0% of the time, Pallas kernels for 13%

commit v1 on v0

--- a/solution.py
+++ b/solution.py
@@ -77,11 +77,11 @@
     return near + jnp.where(lanes == C - 1, 0.0, pltpu.roll(centre, C - 1, 1))
 
 
-def sweep_planes(src, dst, weight, supply, z, depth, block):
+def sweep_planes(src, dst, weight, supply, z, depth, block, rows=None):
     lanes = lane_of((block, C))
     low = lanes == 0
     high = lanes == C - 1
-    for x in range(0, C, block):
+    for x in range(0, C, block) if rows is None else rows:
         r = PAD + x
         column = [src[z + j, r : r + block, :] for j in range(depth + 2)]
         for j in range(depth):
@@ -93,11 +93,7 @@
 
 
 def sweep(src, dst, weight, supply):
-    def planes(i, carry):
-        sweep_planes(src, dst, weight, supply, i * WIDE, WIDE, 8)
-        return carry
-
-    lax.fori_loop(0, CZ // WIDE, planes, 0)
+    sweep_planes(src, dst, weight, supply, 0, CZ, 8)
 
 
 def row_layer(src, base, at, out):
@@ -381,26 +377,38 @@
 
 def response_kernel(*refs):
     lifted = refs[:6]
-    weight, resp, sums, lift, mid, turn, cols = refs[6:]
+    low_y, high_y, weight, wx, wy, resp, sums, lift, mid, turn, cols = refs[6:]
+    layers = lift_layers(lifted, turn, False)
+    sums[...] = row_of_sums([square_sum(lifted, lifted), layer_energy(layers, layers, layer_weights(weight, wx, wy))])
     cols[...] = pack_columns(turn, lifted[2][...], lifted[3][...])
-
-    def plane(z, carry):
-        lift[z] = column_plane(cols[...], z)
-        return carry
-
-    lax.fori_loop(0, CZ, plane, 0, unroll=WIDE)
-    add_rows(lift, lifted, 1.0)
+    turn[layer_rows(0), :] = wy[2] * (wy[3] * lifted[3][...])
+    turn[layer_rows(1), :] = high_y[CZ:, :]
+    turn[layer_rows(2), :] = low_y[CZ:, :]
+    turn[layer_rows(3), :] = wy[1] * (wy[0] * lifted[2][...])
+    turn[...] = turn[...].T
     zero_ends(mid)
     zero_ends(resp)
-
-    def scale(z, acc):
-        once = weight[z] * lift[z]
-        mid[z + 1, INNER, :] = once
-        return acc + fold(once * lift[z])
-
-    acc = lax.fori_loop(0, CZ, scale, jnp.zeros((8, C), F32), unroll=UNROLL)
-    sweep(mid, resp, weight, lift)
-    sums[...] = row_of_sums([square_sum(lifted, lifted), jnp.sum(acc) / DAMPING_WEIGHT])
+    lanes = lane_of((C, C))
+    beside = (lanes < 2) | (lanes >= C - 2)
+
+    def plane(z, carry):
+        resp[z + 1, INNER, :] = jnp.where(beside, pltpu.roll(turn[...], C - 2 - 4 * z, 1), 0.0)
+        return carry
+
+    lax.fori_loop(0, CZ, plane, 0, unroll=WIDE)
+    near_x = ((0, 16), (C - 16, C))
+    near_z = (0, 1, 2, CZ - 3, CZ - 2, CZ - 1)
+    edge = (lanes == 0) | (lanes == C - 1)
+    for z in range(CZ):
+        for a, b in ((0, C),) if z in near_z else near_x:
+            lift[z, a:b, :] = jnp.where(edge[a:b], pltpu.roll(cols[a:b, :], C - 2 - 4 * z, 1), 0.0)
+    add_rows(lift, lifted, 1.0)
+    for z in range(CZ):
+        for a, b in ((0, C),) if z in near_z else near_x:
+            mid[z + 1, PAD + a : PAD + b, :] = weight[z, a:b, :] * lift[z, a:b, :]
+    sweep_planes(mid, resp, weight, lift, 0, CZ, 8, (0, C - 8))
+    for z in (0, CZ - 2):
+        sweep_planes(mid, resp, weight, lift, z, 2, 8, range(8, C - 8, 8))
 
 
 def merge_sides(low, high):
@@ -594,7 +602,8 @@
         if first:
             prev = out[17:]
         got = exchange(sends)
-        resp, sums = call(response_kernel, [PADDED, ROW], [S_FIELD, S_PADDED, S_SQUARE, S_SQUARE], lift_1 + [weight], 3)
+        args = lift_1 + own_uv[2:4] + [weight, wx, wy]
+        resp, sums = call(response_kernel, [PADDED, ROW], [S_FIELD, S_PADDED, S_SQUARE, S_SQUARE], args, 3)
         args = own_uv + got + [bases] + prev + [weight, wx, wy, sums]
         outs = SIDE + SIDE + [SQUARE] + (SIDE + SIDE if first else [])
         scratch = ([] if first else S_SIDE + S_SIDE) + [pltpu.VMEM((2, C, C), F32)]

time: 88.2 us -> 87.5 us (level)
  Pallas kernels: 27.8 us -> 25.4 us
  blocking collectives: 37.6 us -> 38.9 us
    pallas_call x11, Pallas kernels: 27.8 us -> 25.4 us  [call(): pl.pallas_call(kernel, out_shape=tuple(outs), in_specs=in_specs or [VM] *...]
    all_to_all x2, blocking collectives: 37.6 us -> 38.9 us  [gather_rows(): rows = lax.all_to_all(rows.reshape(C, 1, C), AXES, 0, 0)]
  transfers between devices with their start and end apart: 20 -> 20, of which waited for: 0 -> 2; matrix products, arithmetic and copies ran while one was open for 0% -> 0% of each run, Pallas kernels for 13% -> 11%
where the time goes in v1:
time: 87.5 us; the launch traced here: 87.4 us
  blocking collectives  38.9 us (44%)
  Pallas kernels  25.4 us (29%)
  starting transfers between devices  21.6 us (25%)
  between operations  0.97 us (1%)
    all_to_all x2, blocking collectives, gather_rows(): rows = lax.all_to_all(rows.reshape(C, 1, C), AXES, 0, 0)  38.9 us
    pallas_call x11, Pallas kernels, call(): pl.pallas_call(kernel, out_shape=tuple(outs), in_specs=in_specs or [VM] *...  25.4 us
    ppermute x4, starting transfers between devices, exchange(): zz = lax.ppermute(zz, 'gz', [(0, 1), (1, 0)])  6.88 us
    ppermute x4, starting transfers between devices, exchange(): yb = lax.ppermute(yb, both, swap_pairs('y', 1))  5.99 us
    ppermute x4, starting transfers between devices, exchange(): xa = lax.ppermute(xa, both, swap_pairs('x', 0))  4.95 us
    ppermute x4, starting transfers between devices, exchange(): xb = lax.ppermute(xb, both, swap_pairs('x', 1))  3.77 us
  transfers between devices with their start and end apart: 20, of which 2 were waited for; matrix products, arithmetic and copies ran while one was open for 0% of the time, Pallas kernels for 11%

profile of v1, /device:TPU:1, one launch (start us, length us, event | category | flops | bytes accessed | tf_op | source)
XLA Modules:
  0.0 87.4 jit_solution(13078287998977320865)
XLA Ops:
  0.6 4.5 %shard_map.75 = (f32[32,128,128]{2,1,0:T(8,128)S(1)}, f32[34,144,128]{2,1,0:T(8,128)S(1)}, bf16[3,128,384]{2,1,0:T(8,128)(2,1)S(1)}, f32[32,128,128]{2,1,0:T(8,1...) custom-call(f32[32,128,128]{2,1,0:T(8,128)} %heat_in.1, ...), custom_call_target="tpu_custom_call" | custom-call | flops 40000000 | bytes 1048576 | tf_op jit(solution)/shard_map/pallas_call | solution.py:536
  5.2 3.6 %collective-permute-start.4 = (f32[256,128]{1,0:T(8,128)S(1)}, f32[256,128]{1,0:T(8,128)S(1)}, u32[]{:S(2)}, u32[]{:S(2)}) collective-permute-start(f32[256,128]{1,0:T(8,128)S(1)} %get-tuple-element.125), channel_id=1, source_target_pairs={{0,1},{1,0},{2,3},{3,2},{4,5},{5,4},{6,7},{7,6},{8,9},{9,8},{10,11... | collective-permute-start | bytes 393224 | tf_op jit(solution)/shard_map/ppermute | solution.py:569
  8.8 1.3 %collective-permute-start = (f32[160,128]{1,0:T(8,128)S(1)}, f32[160,128]{1,0:T(8,128)S(1)}, u32[]{:S(2)}, u32[]{:S(2)}) collective-permute-start(f32[160,128]{1,0:T(8,128)S(1)} %get-tuple-element.121), channel_id=1, source_target_pairs={{0,32},{2,34},{4,36},{6,38},{8,40},{10,42},{12,44},{14,46},{16,48}... | collective-permute-start | bytes 245768 | tf_op jit(solution)/shard_map/ppermute | solution.py:567
  10.1 1.2 %collective-permute-start.1 = (f32[160,128]{1,0:T(8,128)S(1)}, f32[160,128]{1,0:T(8,128)S(1)}, u32[]{:S(2)}, u32[]{:S(2)}) collective-permute-start(f32[160,128]{1,0:T(8,128)S(1)} %get-tuple-element.122), channel_id=1, source_target_pairs={{0,2},{2,0},{4,6},{6,4},{8,10},{10,8},{12,14},{14,12},{16,18},{18,... | collective-permute-start | bytes 245768 | tf_op jit(solution)/shard_map/ppermute | solution.py:570
  11.4 2.0 %collective-permute-start.3 = (f32[160,128]{1,0:T(8,128)S(1)}, f32[160,128]{1,0:T(8,128)S(1)}, u32[]{:S(2)}, u32[]{:S(2)}) collective-permute-start(f32[160,128]{1,0:T(8,128)S(1)} %get-tuple-element.124), channel_id=1, source_target_pairs={{0,32},{2,4},{4,2},{6,8},{8,6},{10,12},{12,10},{14,16},{16,14},{18... | collective-permute-start | bytes 245768 | tf_op jit(solution)/shard_map/ppermute | solution.py:568
  13.4 2.9 %shard_map.76 = (f32[34,144,128]{2,1,0:T(8,128)S(1)}, f32[32,128]{1,0:T(8,128)S(1)}, f32[32,128]{1,0:T(8,128)S(1)}, f32[32,128]{1,0:T(8,128)S(1)}, f32[32,128]{1...) custom-call(f32[34,144,128]{2,1,0:T(8,128)S(1)} %get-tuple-element.130.state, ...), custom_call_target="tpu_custom_call" | custom-call | flops 30000000 | bytes 1048576 | tf_op jit(solution)/shard_map/pallas_call | solution.py:536
  16.3 1.2 %shard_map.77 = (f32[32,128]{1,0:T(8,128)S(1)}, f32[32,128]{1,0:T(8,128)S(1)}, f32[32,128]{1,0:T(8,128)S(1)}, f32[32,128]{1,0:T(8,128)S(1)}, f32[128,128]{1,0:T(...) custom-call(f32[32,128]{1,0:T(8,128)S(1)} %get-tuple-element.115.ref, ...), custom_call_target="tpu_custom_call" | custom-call | flops 20000000 | bytes 1048576 | tf_op jit(solution)/shard_map/pallas_call | solution.py:536
  17.6 0.3 collective-permute-start.9
  17.9 2.1 %collective-permute-start.5 = (f32[64,128]{1,0:T(8,128)S(1)}, f32[64,128]{1,0:T(8,128)S(1)}, u32[]{:S(2)}, u32[]{:S(2)}) collective-permute-start(f32[64,128]{1,0:T(8,128)S(1)} %get-tuple-element.144), channel_id=1, source_target_pairs={{0,32},{2,34},{4,36},{6,38},{8,40},{10,42},{12,44},{14,46},{16,48}... | collective-permute-start | bytes 98312 | tf_op jit(solution)/shard_map/ppermute | solution.py:567
  19.9 0.5 collective-permute-start.6
  20.4 0.0 collective-permute-start.7
  20.5 1.5 %collective-permute-start.8 = (f32[64,128]{1,0:T(8,128)S(1)}, f32[64,128]{1,0:T(8,128)S(1)}, u32[]{:S(2)}, u32[]{:S(2)}) collective-permute-start(f32[64,128]{1,0:T(8,128)S(1)} %get-tuple-element.147), channel_id=1, source_target_pairs={{0,32},{2,4},{4,2},{6,8},{8,6},{10,12},{12,10},{14,16},{16,14},{18... | collective-permute-start | bytes 98312 | tf_op jit(solution)/shard_map/ppermute | solution.py:568
  22.0 1.7 %shard_map.78 = (f32[34,144,128]{2,1,0:T(8,128)S(1)}, f32[1,128]{1,0:T(1,128)S(1)}) custom-call(f32[32,128]{1,0:T(8,128)S(1)} %get-tuple-element.151.refs_0_.refs_5_, f32[32,128]{1,0:T(8,128)S(1)} %get-tuple-element.152.refs_1_.refs_6_, f32[32,128]{1,0:T(8,128)S(1)} %get-tuple-element.153.refs_2_.refs_7_, f32[32,128]{1,0:T(8,128)S(1)} %get-tuple-element.154.refs_3_.refs_8_, ...), custom_call_target="tpu_custom_call" | custom-call | flops 30000000 | bytes 1048576 | tf_op jit(solution)/shard_map/pallas_call | solution.py:536
  23.7 0.3 collective-permute-done.8.refs_9_
  24.1 1.5 %shard_map.79 = (f32[32,128]{1,0:T(8,128)S(1)}, f32[32,128]{1,0:T(8,128)S(1)}, f32[128,128]{1,0:T(8,128)S(1)}, f32[32,128]{1,0:T(8,128)S(1)}, f32[32,128]{1,0:T(...) custom-call(f32[64,128]{1,0:T(8,128)S(1)} %get-tuple-element.138.ref, ...), custom_call_target="tpu_custom_call" | custom-call | flops 20000000 | bytes 1048576 | tf_op jit(solution)/shard_map/pallas_call | solution.py:536
  25.6 21.4 %all_to_all.10 = f32[128,1,128]{2,1,0:T(1,128)S(1)} all-to-all(f32[128,1,128]{2,1,0:T(1,128)S(1)} %bitcast.15), channel_id=1, replica_groups=mesh['gx'=4,'gy'=16,'gz'=2] {'gx','gy','gz'}, dimensions={0} | all-to-all | bytes 131072 | tf_op jit(solution)/shard_map/all_to_all | solution.py:576
  47.0 4.0 %shard_map.80 = (f32[32,128,128]{2,1,0:T(8,128)S(1)}, f32[34,144,128]{2,1,0:T(8,128)S(1)}, f32[32,128]{1,0:T(8,128)S(1)}, f32[32,128]{1,0:T(8,128)S(1)}, f32[128...) custom-call(f32[128,128]{1,0:T(8,128)S(1)} %bitcast.13, ...), custom_call_target="tpu_custom_call" | custom-call | flops 50000000 | bytes 1048576 | tf_op jit(solution)/shard_map/pallas_call | solution.py:536
  51.0 1.1 %collective-permute-start.14 = (f32[128,128]{1,0:T(8,128)S(1)}, f32[128,128]{1,0:T(8,128)S(1)}, u32[]{:S(2)}, u32[]{:S(2)}) collective-permute-start(f32[128,128]{1,0:T(8,128)S(1)} %get-tuple-element.183), channel_id=1, source_target_pairs={{0,1},{1,0},{2,3},{3,2},{4,5},{5,4},{6,7},{7,6},{8,9},{9,8},{10,11... | collective-permute-start | bytes 196616 | tf_op jit(solution)/shard_map/ppermute | solution.py:569
  52.1 0.4 collective-permute-start.10
  52.5 1.1 %collective-permute-start.11 = (f32[32,128]{1,0:T(8,128)S(1)}, f32[32,128]{1,0:T(8,128)S(1)}, u32[]{:S(2)}, u32[]{:S(2)}) collective-permute-start(f32[32,128]{1,0:T(8,128)S(1)} %get-tuple-element.180), channel_id=1, source_target_pairs={{0,2},{2,0},{4,6},{6,4},{8,10},{10,8},{12,14},{14,12},{16,18},{18,... | collective-permute-start | bytes 49160 | tf_op jit(solution)/shard_map/ppermute | solution.py:570
  53.6 0.9 %collective-permute-start.13 = (f32[32,128]{1,0:T(8,128)S(1)}, f32[32,128]{1,0:T(8,128)S(1)}, u32[]{:S(2)}, u32[]{:S(2)}) collective-permute-start(f32[32,128]{1,0:T(8,128)S(1)} %get-tuple-element.182), channel_id=1, source_target_pairs={{0,32},{2,4},{4,2},{6,8},{8,6},{10,12},{12,10},{14,16},{16,14},{18... | collective-permute-start | bytes 49160 | tf_op jit(solution)/shard_map/ppermute | solution.py:568
  54.5 2.9 %shard_map.81 = (f32[34,144,128]{2,1,0:T(8,128)S(1)}, f32[32,128]{1,0:T(8,128)S(1)}, f32[32,128]{1,0:T(8,128)S(1)}, f32[32,128]{1,0:T(8,128)S(1)}, f32[32,128]{1...) custom-call(f32[34,144,128]{2,1,0:T(8,128)S(1)} %get-tuple-element.184.state, ...), custom_call_target="tpu_custom_call" | custom-call | flops 30000000 | bytes 1048576 | tf_op jit(solution)/shard_map/pallas_call | solution.py:536
  57.5 1.2 %shard_map.82 = (f32[32,128]{1,0:T(8,128)S(1)}, f32[32,128]{1,0:T(8,128)S(1)}, f32[32,128]{1,0:T(8,128)S(1)}, f32[32,128]{1,0:T(8,128)S(1)}, f32[128,128]{1,0:T(...) custom-call(f32[32,128]{1,0:T(8,128)S(1)} %get-tuple-element.173.ref, ...), custom_call_target="tpu_custom_call" | custom-call | flops 20000000 | bytes 1048576 | tf_op jit(solution)/shard_map/pallas_call | solution.py:536
  58.6 1.8 %collective-permute-start.19 = (f32[256,128]{1,0:T(8,128)S(1)}, f32[256,128]{1,0:T(8,128)S(1)}, u32[]{:S(2)}, u32[]{:S(2)}) collective-permute-start(f32[256,128]{1,0:T(8,128)S(1)} %get-tuple-element.202), channel_id=1, source_target_pairs={{0,1},{1,0},{2,3},{3,2},{4,5},{5,4},{6,7},{7,6},{8,9},{9,8},{10,11... | collective-permute-start | bytes 393224 | tf_op jit(solution)/shard_map/ppermute | solution.py:569
  60.4 1.2 %collective-permute-start.15 = (f32[64,128]{1,0:T(8,128)S(1)}, f32[64,128]{1,0:T(8,128)S(1)}, u32[]{:S(2)}, u32[]{:S(2)}) collective-permute-start(f32[64,128]{1,0:T(8,128)S(1)} %get-tuple-element.198), channel_id=1, source_target_pairs={{0,32},{2,34},{4,36},{6,38},{8,40},{10,42},{12,44},{14,46},{16,48}... | collective-permute-start | bytes 98312 | tf_op jit(solution)/shard_map/ppermute | solution.py:567
  61.7 1.0 %collective-permute-start.16 = (f32[64,128]{1,0:T(8,128)S(1)}, f32[64,128]{1,0:T(8,128)S(1)}, u32[]{:S(2)}, u32[]{:S(2)}) collective-permute-start(f32[64,128]{1,0:T(8,128)S(1)} %get-tuple-element.199), channel_id=1, source_target_pairs={{0,2},{2,0},{4,6},{6,4},{8,10},{10,8},{12,14},{14,12},{16,18},{18,... | collective-permute-start | bytes 98312 | tf_op jit(solution)/shard_map/ppermute | solution.py:570
  62.6 1.5 %collective-permute-start.18 = (f32[64,128]{1,0:T(8,128)S(1)}, f32[64,128]{1,0:T(8,128)S(1)}, u32[]{:S(2)}, u32[]{:S(2)}) collective-permute-start(f32[64,128]{1,0:T(8,128)S(1)} %get-tuple-element.201), channel_id=1, source_target_pairs={{0,32},{2,4},{4,2},{6,8},{8,6},{10,12},{12,10},{14,16},{16,14},{18... | collective-permute-start | bytes 98312 | tf_op jit(solution)/shard_map/ppermute | solution.py:568
  64.1 1.7 %shard_map.83 = (f32[34,144,128]{2,1,0:T(8,128)S(1)}, f32[1,128]{1,0:T(1,128)S(1)}) custom-call(f32[32,128]{1,0:T(8,128)S(1)} %get-tuple-element.203.refs_0_, f32[32,128]{1,0:T(8,128)S(1)} %get-tuple-element.204.refs_1_.refs_6_, f32[32,128]{1,0:T(8,128)S(1)} %get-tuple-element.205.refs_2_, f32[32,128]{1,0:T(8,128)S(1)} %get-tuple-element.206.refs_3_.refs_7_, ...), custom_call_target="tpu_custom_call" | custom-call | flops 30000000 | bytes 1048576 | tf_op jit(solution)/shard_map/pallas_call | solution.py:536
  65.9 0.1 collective-permute-done.18.refs_9_
  66.0 1.5 %shard_map.84 = (f32[32,128]{1,0:T(8,128)S(1)}, f32[32,128]{1,0:T(8,128)S(1)}, f32[128,128]{1,0:T(8,128)S(1)}, f32[32,128]{1,0:T(8,128)S(1)}, f32[32,128]{1,0:T(...) custom-call(f32[64,128]{1,0:T(8,128)S(1)} %get-tuple-element.192.refs_0_, ...), custom_call_target="tpu_custom_call" | custom-call | flops 20000000 | bytes 1048576 | tf_op jit(solution)/shard_map/pallas_call | solution.py:536
  67.5 17.6 %all_to_all.11 = f32[128,1,128]{2,1,0:T(1,128)S(1)} all-to-all(f32[128,1,128]{2,1,0:T(1,128)S(1)} %bitcast.16), channel_id=1, replica_groups=mesh['gx'=4,'gy'=16,'gz'=2] {'gx','gy','gz'}, dimensions={0} | all-to-all | bytes 131072 | tf_op jit(solution)/shard_map/all_to_all | solution.py:576
  85.0 2.2 %shard_map.85 = (f32[32,128,128]{2,1,0:T(8,128)}, f32[32,128]{1,0:T(8,128)}, f32[32,128]{1,0:T(8,128)}, f32[128,128]{1,0:T(8,128)}) custom-call(f32[128,128]{1,0:T(8,128)S(1)} %bitcast.14, f32[34,144,128]{2,1,0:T(8,128)S(1)} %get-tuple-element.211.refs_1_, f32[34,144,128]{2,1,0:T(8,128)S(1)} %get-tuple-element.212.refs_2_, ...), custom_call_target="tpu_custom_call" | custom-call | flops 20000000 | bytes 1048576 | tf_op jit(solution)/shard_map/pallas_call | solution.py:536
  (21 shorter events, 0.1 us)
Async XLA Ops:
  5.2 11.2 %collective-permute-start.4 = (f32[256,128]{1,0:T(8,128)S(1)}, f32[256,128]{1,0:T(8,128)S(1)}, u32[]{:S(2)}, u32[]{:S(2)}) collective-permute-start(f32[256,128]{1,0:T(8,128)S(1)} %get-tuple-element.125), channel_id=1, source_target_pairs={{0,1},{1,0},{2,3},{3,2},{4,5},{5,4},{6,7},{7,6},{8,9},{9,8},{10,11... | collective-permute-start | bytes 393224 | tf_op jit(solution)/shard_map/ppermute | solution.py:569
  8.8 7.5 %collective-permute-start = (f32[160,128]{1,0:T(8,128)S(1)}, f32[160,128]{1,0:T(8,128)S(1)}, u32[]{:S(2)}, u32[]{:S(2)}) collective-permute-start(f32[160,128]{1,0:T(8,128)S(1)} %get-tuple-element.121), channel_id=1, source_target_pairs={{0,32},{2,34},{4,36},{6,38},{8,40},{10,42},{12,44},{14,46},{16,48}... | collective-permute-start | bytes 245768 | tf_op jit(solution)/shard_map/ppermute | solution.py:567
  10.1 6.2 %collective-permute-start.1 = (f32[160,128]{1,0:T(8,128)S(1)}, f32[160,128]{1,0:T(8,128)S(1)}, u32[]{:S(2)}, u32[]{:S(2)}) collective-permute-start(f32[160,128]{1,0:T(8,128)S(1)} %get-tuple-element.122), channel_id=1, source_target_pairs={{0,2},{2,0},{4,6},{6,4},{8,10},{10,8},{12,14},{14,12},{16,18},{18,... | collective-permute-start | bytes 245768 | tf_op jit(solution)/shard_map/ppermute | solution.py:570
  11.4 5.0 %collective-permute-start.2 = (f32[160,128]{1,0:T(8,128)S(1)}, f32[160,128]{1,0:T(8,128)S(1)}, u32[]{:S(2)}, u32[]{:S(2)}) collective-permute-start(f32[160,128]{1,0:T(8,128)S(1)} %get-tuple-element.123), channel_id=1, source_target_pairs={{0,2},{2,0},{4,6},{6,4},{8,10},{10,8},{12,14},{14,12},{16,18},{18,... | collective-permute-start | bytes 245768 | tf_op jit(solution)/shard_map/ppermute | solution.py:571
  11.4 5.0 %collective-permute-start.3 = (f32[160,128]{1,0:T(8,128)S(1)}, f32[160,128]{1,0:T(8,128)S(1)}, u32[]{:S(2)}, u32[]{:S(2)}) collective-permute-start(f32[160,128]{1,0:T(8,128)S(1)} %get-tuple-element.124), channel_id=1, source_target_pairs={{0,32},{2,4},{4,2},{6,8},{8,6},{10,12},{12,10},{14,16},{16,14},{18... | collective-permute-start | bytes 245768 | tf_op jit(solution)/shard_map/ppermute | solution.py:568
  17.6 6.5 %collective-permute-start.9 = (f32[256,128]{1,0:T(8,128)S(1)}, f32[256,128]{1,0:T(8,128)S(1)}, u32[]{:S(2)}, u32[]{:S(2)}) collective-permute-start(f32[256,128]{1,0:T(8,128)S(1)} %get-tuple-element.148), channel_id=1, source_target_pairs={{0,1},{1,0},{2,3},{3,2},{4,5},{5,4},{6,7},{7,6},{8,9},{9,8},{10,11... | collective-permute-start | bytes 393224 | tf_op jit(solution)/shard_map/ppermute | solution.py:569
  17.9 5.8 %collective-permute-start.5 = (f32[64,128]{1,0:T(8,128)S(1)}, f32[64,128]{1,0:T(8,128)S(1)}, u32[]{:S(2)}, u32[]{:S(2)}) collective-permute-start(f32[64,128]{1,0:T(8,128)S(1)} %get-tuple-element.144), channel_id=1, source_target_pairs={{0,32},{2,34},{4,36},{6,38},{8,40},{10,42},{12,44},{14,46},{16,48}... | collective-permute-start | bytes 98312 | tf_op jit(solution)/shard_map/ppermute | solution.py:567
  19.9 3.8 %collective-permute-start.6 = (f32[64,128]{1,0:T(8,128)S(1)}, f32[64,128]{1,0:T(8,128)S(1)}, u32[]{:S(2)}, u32[]{:S(2)}) collective-permute-start(f32[64,128]{1,0:T(8,128)S(1)} %get-tuple-element.145), channel_id=1, source_target_pairs={{0,2},{2,0},{4,6},{6,4},{8,10},{10,8},{12,14},{14,12},{16,18},{18,... | collective-permute-start | bytes 98312 | tf_op jit(solution)/shard_map/ppermute | solution.py:570
  20.4 3.3 %collective-permute-start.7 = (f32[64,128]{1,0:T(8,128)S(1)}, f32[64,128]{1,0:T(8,128)S(1)}, u32[]{:S(2)}, u32[]{:S(2)}) collective-permute-start(f32[64,128]{1,0:T(8,128)S(1)} %get-tuple-element.146), channel_id=1, source_target_pairs={{0,2},{2,0},{4,6},{6,4},{8,10},{10,8},{12,14},{14,12},{16,18},{18,... | collective-permute-start | bytes 98312 | tf_op jit(solution)/shard_map/ppermute | solution.py:571
  20.5 3.6 %collective-permute-start.8 = (f32[64,128]{1,0:T(8,128)S(1)}, f32[64,128]{1,0:T(8,128)S(1)}, u32[]{:S(2)}, u32[]{:S(2)}) collective-permute-start(f32[64,128]{1,0:T(8,128)S(1)} %get-tuple-element.147), channel_id=1, source_target_pairs={{0,32},{2,4},{4,2},{6,8},{8,6},{10,12},{12,10},{14,16},{16,14},{18... | collective-permute-start | bytes 98312 | tf_op jit(solution)/shard_map/ppermute | solution.py:568
  51.0 6.5 %collective-permute-start.14 = (f32[128,128]{1,0:T(8,128)S(1)}, f32[128,128]{1,0:T(8,128)S(1)}, u32[]{:S(2)}, u32[]{:S(2)}) collective-permute-start(f32[128,128]{1,0:T(8,128)S(1)} %get-tuple-element.183), channel_id=1, source_target_pairs={{0,1},{1,0},{2,3},{3,2},{4,5},{5,4},{6,7},{7,6},{8,9},{9,8},{10,11... | collective-permute-start | bytes 196616 | tf_op jit(solution)/shard_map/ppermute | solution.py:569
  52.1 5.3 %collective-permute-start.10 = (f32[32,128]{1,0:T(8,128)S(1)}, f32[32,128]{1,0:T(8,128)S(1)}, u32[]{:S(2)}, u32[]{:S(2)}) collective-permute-start(f32[32,128]{1,0:T(8,128)S(1)} %get-tuple-element.179), channel_id=1, source_target_pairs={{0,32},{2,34},{4,36},{6,38},{8,40},{10,42},{12,44},{14,46},{16,48}... | collective-permute-start | bytes 49160 | tf_op jit(solution)/shard_map/ppermute | solution.py:567
  52.5 5.0 %collective-permute-start.11 = (f32[32,128]{1,0:T(8,128)S(1)}, f32[32,128]{1,0:T(8,128)S(1)}, u32[]{:S(2)}, u32[]{:S(2)}) collective-permute-start(f32[32,128]{1,0:T(8,128)S(1)} %get-tuple-element.180), channel_id=1, source_target_pairs={{0,2},{2,0},{4,6},{6,4},{8,10},{10,8},{12,14},{14,12},{16,18},{18,... | collective-permute-start | bytes 49160 | tf_op jit(solution)/shard_map/ppermute | solution.py:570
  53.6 3.9 %collective-permute-start.12 = (f32[32,128]{1,0:T(8,128)S(1)}, f32[32,128]{1,0:T(8,128)S(1)}, u32[]{:S(2)}, u32[]{:S(2)}) collective-permute-start(f32[32,128]{1,0:T(8,128)S(1)} %get-tuple-element.181), channel_id=1, source_target_pairs={{0,2},{2,0},{4,6},{6,4},{8,10},{10,8},{12,14},{14,12},{16,18},{18,... | collective-permute-start | bytes 49160 | tf_op jit(solution)/shard_map/ppermute | solution.py:571
  53.6 3.9 %collective-permute-start.13 = (f32[32,128]{1,0:T(8,128)S(1)}, f32[32,128]{1,0:T(8,128)S(1)}, u32[]{:S(2)}, u32[]{:S(2)}) collective-permute-start(f32[32,128]{1,0:T(8,128)S(1)} %get-tuple-element.182), channel_id=1, source_target_pairs={{0,32},{2,4},{4,2},{6,8},{8,6},{10,12},{12,10},{14,16},{16,14},{18... | collective-permute-start | bytes 49160 | tf_op jit(solution)/shard_map/ppermute | solution.py:568
  58.6 7.3 %collective-permute-start.19 = (f32[256,128]{1,0:T(8,128)S(1)}, f32[256,128]{1,0:T(8,128)S(1)}, u32[]{:S(2)}, u32[]{:S(2)}) collective-permute-start(f32[256,128]{1,0:T(8,128)S(1)} %get-tuple-element.202), channel_id=1, source_target_pairs={{0,1},{1,0},{2,3},{3,2},{4,5},{5,4},{6,7},{7,6},{8,9},{9,8},{10,11... | collective-permute-start | bytes 393224 | tf_op jit(solution)/shard_map/ppermute | solution.py:569
  60.4 5.4 %collective-permute-start.15 = (f32[64,128]{1,0:T(8,128)S(1)}, f32[64,128]{1,0:T(8,128)S(1)}, u32[]{:S(2)}, u32[]{:S(2)}) collective-permute-start(f32[64,128]{1,0:T(8,128)S(1)} %get-tuple-element.198), channel_id=1, source_target_pairs={{0,32},{2,34},{4,36},{6,38},{8,40},{10,42},{12,44},{14,46},{16,48}... | collective-permute-start | bytes 98312 | tf_op jit(solution)/shard_map/ppermute | solution.py:567
  61.7 4.2 %collective-permute-start.16 = (f32[64,128]{1,0:T(8,128)S(1)}, f32[64,128]{1,0:T(8,128)S(1)}, u32[]{:S(2)}, u32[]{:S(2)}) collective-permute-start(f32[64,128]{1,0:T(8,128)S(1)} %get-tuple-element.199), channel_id=1, source_target_pairs={{0,2},{2,0},{4,6},{6,4},{8,10},{10,8},{12,14},{14,12},{16,18},{18,... | collective-permute-start | bytes 98312 | tf_op jit(solution)/shard_map/ppermute | solution.py:570
  62.6 3.3 %collective-permute-start.17 = (f32[64,128]{1,0:T(8,128)S(1)}, f32[64,128]{1,0:T(8,128)S(1)}, u32[]{:S(2)}, u32[]{:S(2)}) collective-permute-start(f32[64,128]{1,0:T(8,128)S(1)} %get-tuple-element.200), channel_id=1, source_target_pairs={{0,2},{2,0},{4,6},{6,4},{8,10},{10,8},{12,14},{14,12},{16,18},{18,... | collective-permute-start | bytes 98312 | tf_op jit(solution)/shard_map/ppermute | solution.py:571
  62.6 3.3 %collective-permute-start.18 = (f32[64,128]{1,0:T(8,128)S(1)}, f32[64,128]{1,0:T(8,128)S(1)}, u32[]{:S(2)}, u32[]{:S(2)}) collective-permute-start(f32[64,128]{1,0:T(8,128)S(1)} %get-tuple-element.201), channel_id=1, source_target_pairs={{0,32},{2,4},{4,2},{6,8},{8,6},{10,12},{12,10},{14,16},{16,14},{18... | collective-permute-start | bytes 98312 | tf_op jit(solution)/shard_map/ppermute | solution.py:568

commit v2 on v1

--- a/solution.py
+++ b/solution.py
@@ -209,7 +209,7 @@
         for e in (0, last):
             t = layers_a[e] * layers_b[e] * w[e]
             acc = acc + fold(t if mask is None else jnp.where(mask, t, 0.0))
-    return jnp.sum(acc) / DAMPING_WEIGHT
+    return acc * (1.0 / DAMPING_WEIGHT)
 
 
 def places():
@@ -332,15 +332,16 @@
 
 
 def square_sum(a, b):
-    return jnp.sum(sum(fold(a[i][...] * b[i][...]) for i in (1, 3, 5)))
-
-
-def row_of_sums(values):
-    lanes = lane_of((1, C))
-    row = jnp.zeros((1, C), F32)
-    for i, v in enumerate(values):
-        row = jnp.where(lanes == i, v, row)
-    return row
+    return sum(fold(a[i][...] * b[i][...]) for i in (1, 3, 5))
+
+
+def row_of_sums(partials, base):
+    rows = row_of((8, C))
+    stacked = jnp.zeros((8, C), F32)
+    for i, p in enumerate(partials):
+        stacked = jnp.where(rows == base + i, jnp.sum(p, axis=0, keepdims=True), stacked)
+    totals = jnp.sum(stacked, axis=1, keepdims=True)
+    return jnp.sum(jnp.where(lane_of((8, C)) == rows, totals, 0.0), axis=0, keepdims=True)
 
 
 def second_kernel(first, *refs):
@@ -379,7 +380,7 @@
     lifted = refs[:6]
     low_y, high_y, weight, wx, wy, resp, sums, lift, mid, turn, cols = refs[6:]
     layers = lift_layers(lifted, turn, False)
-    sums[...] = row_of_sums([square_sum(lifted, lifted), layer_energy(layers, layers, layer_weights(weight, wx, wy))])
+    sums[...] = row_of_sums([square_sum(lifted, lifted), layer_energy(layers, layers, layer_weights(weight, wx, wy))], 0)
     cols[...] = pack_columns(turn, lifted[2][...], lifted[3][...])
     turn[layer_rows(0), :] = wy[2] * (wy[3] * lifted[3][...])
     turn[layer_rows(1), :] = high_y[CZ:, :]
@@ -433,10 +434,7 @@
     v = lift_layers(lift_v, turn.at[1], False)
     sums = [square_sum(lift_u, lift_u), square_sum(lift_u, lift_v), square_sum(lift_v, lift_v)]
     sums += [layer_energy(u, u, weights), layer_energy(u, v, weights), layer_energy(v, v, weights)]
-    lanes = lane_of((1, C))
-    row = row_of_sums([0.0, 0.0] + sums)
-    row = jnp.where(lanes < 2, before[...], row)
-    rows[...] = jnp.broadcast_to(row, (C, C))
+    rows[...] = jnp.broadcast_to(before[...] + row_of_sums(sums, 2), (C, C))
 
 
 def steps(totals):

time: 87.5 us -> 87.5 us (level)
  no operation moved by 1% of the time
where the time goes in v2:
time: 87.5 us; the launch traced here: 87.3 us
  blocking collectives  38.9 us (44%)
  Pallas kernels  25.3 us (29%)
  starting transfers between devices  21.6 us (25%)
  between operations  0.96 us (1%)
    all_to_all x2, blocking collectives, gather_rows(): rows = lax.all_to_all(rows.reshape(C, 1, C), AXES, 0, 0)  38.9 us
    pallas_call x11, Pallas kernels, call(): pl.pallas_call(kernel, out_shape=tuple(outs), in_specs=in_specs or [VM] *...  25.3 us
    ppermute x4, starting transfers between devices, exchange(): zz = lax.ppermute(zz, 'gz', [(0, 1), (1, 0)])  6.88 us
    ppermute x4, starting transfers between devices, exchange(): yb = lax.ppermute(yb, both, swap_pairs('y', 1))  5.99 us
    ppermute x4, starting transfers between devices, exchange(): xa = lax.ppermute(xa, both, swap_pairs('x', 0))  4.95 us
    ppermute x4, starting transfers between devices, exchange(): xb = lax.ppermute(xb, both, swap_pairs('x', 1))  3.78 us
  transfers between devices with their start and end apart: 20, of which 2 were waited for; matrix products, arithmetic and copies ran while one was open for 0% of the time, Pallas kernels for 11%

profile of v2, /device:TPU:1, one launch (start us, length us, event | category | flops | bytes accessed | tf_op | source)
XLA Modules:
  0.0 87.3 jit_solution(11613004227049787781)
XLA Ops:
  0.6 4.5 %shard_map.75 = (f32[32,128,128]{2,1,0:T(8,128)S(1)}, f32[34,144,128]{2,1,0:T(8,128)S(1)}, bf16[3,128,384]{2,1,0:T(8,128)(2,1)S(1)}, f32[32,128,128]{2,1,0:T(8,1...) custom-call(f32[32,128,128]{2,1,0:T(8,128)} %heat_in.1, ...), custom_call_target="tpu_custom_call" | custom-call | flops 40000000 | bytes 1048576 | tf_op jit(solution)/shard_map/pallas_call | solution.py:534
  5.2 3.6 %collective-permute-start.4 = (f32[256,128]{1,0:T(8,128)S(1)}, f32[256,128]{1,0:T(8,128)S(1)}, u32[]{:S(2)}, u32[]{:S(2)}) collective-permute-start(f32[256,128]{1,0:T(8,128)S(1)} %get-tuple-element.125), channel_id=1, source_target_pairs={{0,1},{1,0},{2,3},{3,2},{4,5},{5,4},{6,7},{7,6},{8,9},{9,8},{10,11... | collective-permute-start | bytes 393224 | tf_op jit(solution)/shard_map/ppermute | solution.py:567
  8.8 1.3 %collective-permute-start = (f32[160,128]{1,0:T(8,128)S(1)}, f32[160,128]{1,0:T(8,128)S(1)}, u32[]{:S(2)}, u32[]{:S(2)}) collective-permute-start(f32[160,128]{1,0:T(8,128)S(1)} %get-tuple-element.121), channel_id=1, source_target_pairs={{0,32},{2,34},{4,36},{6,38},{8,40},{10,42},{12,44},{14,46},{16,48}... | collective-permute-start | bytes 245768 | tf_op jit(solution)/shard_map/ppermute | solution.py:565
  10.1 1.2 %collective-permute-start.1 = (f32[160,128]{1,0:T(8,128)S(1)}, f32[160,128]{1,0:T(8,128)S(1)}, u32[]{:S(2)}, u32[]{:S(2)}) collective-permute-start(f32[160,128]{1,0:T(8,128)S(1)} %get-tuple-element.122), channel_id=1, source_target_pairs={{0,2},{2,0},{4,6},{6,4},{8,10},{10,8},{12,14},{14,12},{16,18},{18,... | collective-permute-start | bytes 245768 | tf_op jit(solution)/shard_map/ppermute | solution.py:568
  11.4 2.0 %collective-permute-start.3 = (f32[160,128]{1,0:T(8,128)S(1)}, f32[160,128]{1,0:T(8,128)S(1)}, u32[]{:S(2)}, u32[]{:S(2)}) collective-permute-start(f32[160,128]{1,0:T(8,128)S(1)} %get-tuple-element.124), channel_id=1, source_target_pairs={{0,32},{2,4},{4,2},{6,8},{8,6},{10,12},{12,10},{14,16},{16,14},{18... | collective-permute-start | bytes 245768 | tf_op jit(solution)/shard_map/ppermute | solution.py:566
  13.4 2.9 %shard_map.76 = (f32[34,144,128]{2,1,0:T(8,128)S(1)}, f32[32,128]{1,0:T(8,128)S(1)}, f32[32,128]{1,0:T(8,128)S(1)}, f32[32,128]{1,0:T(8,128)S(1)}, f32[32,128]{1...) custom-call(f32[34,144,128]{2,1,0:T(8,128)S(1)} %get-tuple-element.130.state, ...), custom_call_target="tpu_custom_call" | custom-call | flops 30000000 | bytes 1048576 | tf_op jit(solution)/shard_map/pallas_call | solution.py:534
  16.3 1.2 %shard_map.77 = (f32[32,128]{1,0:T(8,128)S(1)}, f32[32,128]{1,0:T(8,128)S(1)}, f32[32,128]{1,0:T(8,128)S(1)}, f32[32,128]{1,0:T(8,128)S(1)}, f32[128,128]{1,0:T(...) custom-call(f32[32,128]{1,0:T(8,128)S(1)} %get-tuple-element.115.ref, ...), custom_call_target="tpu_custom_call" | custom-call | flops 20000000 | bytes 1048576 | tf_op jit(solution)/shard_map/pallas_call | solution.py:534
  17.6 0.3 collective-permute-start.9
  17.9 2.1 %collective-permute-start.5 = (f32[64,128]{1,0:T(8,128)S(1)}, f32[64,128]{1,0:T(8,128)S(1)}, u32[]{:S(2)}, u32[]{:S(2)}) collective-permute-start(f32[64,128]{1,0:T(8,128)S(1)} %get-tuple-element.144), channel_id=1, source_target_pairs={{0,32},{2,34},{4,36},{6,38},{8,40},{10,42},{12,44},{14,46},{16,48}... | collective-permute-start | bytes 98312 | tf_op jit(solution)/shard_map/ppermute | solution.py:565
  19.9 0.5 collective-permute-start.6
  20.4 0.0 collective-permute-start.7
  20.5 1.5 %collective-permute-start.8 = (f32[64,128]{1,0:T(8,128)S(1)}, f32[64,128]{1,0:T(8,128)S(1)}, u32[]{:S(2)}, u32[]{:S(2)}) collective-permute-start(f32[64,128]{1,0:T(8,128)S(1)} %get-tuple-element.147), channel_id=1, source_target_pairs={{0,32},{2,4},{4,2},{6,8},{8,6},{10,12},{12,10},{14,16},{16,14},{18... | collective-permute-start | bytes 98312 | tf_op jit(solution)/shard_map/ppermute | solution.py:566
  22.0 1.7 %shard_map.78 = (f32[34,144,128]{2,1,0:T(8,128)S(1)}, f32[1,128]{1,0:T(1,128)S(1)}) custom-call(f32[32,128]{1,0:T(8,128)S(1)} %get-tuple-element.151.refs_0_.refs_5_, f32[32,128]{1,0:T(8,128)S(1)} %get-tuple-element.152.refs_1_.refs_6_, f32[32,128]{1,0:T(8,128)S(1)} %get-tuple-element.153.refs_2_.refs_7_, f32[32,128]{1,0:T(8,128)S(1)} %get-tuple-element.154.refs_3_.refs_8_, ...), custom_call_target="tpu_custom_call" | custom-call | flops 30000000 | bytes 1048576 | tf_op jit(solution)/shard_map/pallas_call | solution.py:534
  23.7 0.4 collective-permute-done.8.refs_9_
  24.1 1.5 %shard_map.79 = (f32[32,128]{1,0:T(8,128)S(1)}, f32[32,128]{1,0:T(8,128)S(1)}, f32[128,128]{1,0:T(8,128)S(1)}, f32[32,128]{1,0:T(8,128)S(1)}, f32[32,128]{1,0:T(...) custom-call(f32[64,128]{1,0:T(8,128)S(1)} %get-tuple-element.138.ref, ...), custom_call_target="tpu_custom_call" | custom-call | flops 20000000 | bytes 1048576 | tf_op jit(solution)/shard_map/pallas_call | solution.py:534
  25.6 21.4 %all_to_all.10 = f32[128,1,128]{2,1,0:T(1,128)S(1)} all-to-all(f32[128,1,128]{2,1,0:T(1,128)S(1)} %bitcast.15), channel_id=1, replica_groups=mesh['gx'=4,'gy'=16,'gz'=2] {'gx','gy','gz'}, dimensions={0} | all-to-all | bytes 131072 | tf_op jit(solution)/shard_map/all_to_all | solution.py:574
  46.9 4.0 %shard_map.80 = (f32[32,128,128]{2,1,0:T(8,128)S(1)}, f32[34,144,128]{2,1,0:T(8,128)S(1)}, f32[32,128]{1,0:T(8,128)S(1)}, f32[32,128]{1,0:T(8,128)S(1)}, f32[128...) custom-call(f32[128,128]{1,0:T(8,128)S(1)} %bitcast.13, ...), custom_call_target="tpu_custom_call" | custom-call | flops 50000000 | bytes 1048576 | tf_op jit(solution)/shard_map/pallas_call | solution.py:534
  51.0 1.1 %collective-permute-start.14 = (f32[128,128]{1,0:T(8,128)S(1)}, f32[128,128]{1,0:T(8,128)S(1)}, u32[]{:S(2)}, u32[]{:S(2)}) collective-permute-start(f32[128,128]{1,0:T(8,128)S(1)} %get-tuple-element.183), channel_id=1, source_target_pairs={{0,1},{1,0},{2,3},{3,2},{4,5},{5,4},{6,7},{7,6},{8,9},{9,8},{10,11... | collective-permute-start | bytes 196616 | tf_op jit(solution)/shard_map/ppermute | solution.py:567
  52.1 0.4 collective-permute-start.10
  52.4 1.1 %collective-permute-start.11 = (f32[32,128]{1,0:T(8,128)S(1)}, f32[32,128]{1,0:T(8,128)S(1)}, u32[]{:S(2)}, u32[]{:S(2)}) collective-permute-start(f32[32,128]{1,0:T(8,128)S(1)} %get-tuple-element.180), channel_id=1, source_target_pairs={{0,2},{2,0},{4,6},{6,4},{8,10},{10,8},{12,14},{14,12},{16,18},{18,... | collective-permute-start | bytes 49160 | tf_op jit(solution)/shard_map/ppermute | solution.py:568
  53.5 0.9 %collective-permute-start.13 = (f32[32,128]{1,0:T(8,128)S(1)}, f32[32,128]{1,0:T(8,128)S(1)}, u32[]{:S(2)}, u32[]{:S(2)}) collective-permute-start(f32[32,128]{1,0:T(8,128)S(1)} %get-tuple-element.182), channel_id=1, source_target_pairs={{0,32},{2,4},{4,2},{6,8},{8,6},{10,12},{12,10},{14,16},{16,14},{18... | collective-permute-start | bytes 49160 | tf_op jit(solution)/shard_map/ppermute | solution.py:566
  54.5 2.9 %shard_map.81 = (f32[34,144,128]{2,1,0:T(8,128)S(1)}, f32[32,128]{1,0:T(8,128)S(1)}, f32[32,128]{1,0:T(8,128)S(1)}, f32[32,128]{1,0:T(8,128)S(1)}, f32[32,128]{1...) custom-call(f32[34,144,128]{2,1,0:T(8,128)S(1)} %get-tuple-element.184.state, ...), custom_call_target="tpu_custom_call" | custom-call | flops 30000000 | bytes 1048576 | tf_op jit(solution)/shard_map/pallas_call | solution.py:534
  57.4 1.2 %shard_map.82 = (f32[32,128]{1,0:T(8,128)S(1)}, f32[32,128]{1,0:T(8,128)S(1)}, f32[32,128]{1,0:T(8,128)S(1)}, f32[32,128]{1,0:T(8,128)S(1)}, f32[128,128]{1,0:T(...) custom-call(f32[32,128]{1,0:T(8,128)S(1)} %get-tuple-element.173.ref, ...), custom_call_target="tpu_custom_call" | custom-call | flops 20000000 | bytes 1048576 | tf_op jit(solution)/shard_map/pallas_call | solution.py:534
  58.6 1.8 %collective-permute-start.19 = (f32[256,128]{1,0:T(8,128)S(1)}, f32[256,128]{1,0:T(8,128)S(1)}, u32[]{:S(2)}, u32[]{:S(2)}) collective-permute-start(f32[256,128]{1,0:T(8,128)S(1)} %get-tuple-element.202), channel_id=1, source_target_pairs={{0,1},{1,0},{2,3},{3,2},{4,5},{5,4},{6,7},{7,6},{8,9},{9,8},{10,11... | collective-permute-start | bytes 393224 | tf_op jit(solution)/shard_map/ppermute | solution.py:567
  60.4 1.2 %collective-permute-start.15 = (f32[64,128]{1,0:T(8,128)S(1)}, f32[64,128]{1,0:T(8,128)S(1)}, u32[]{:S(2)}, u32[]{:S(2)}) collective-permute-start(f32[64,128]{1,0:T(8,128)S(1)} %get-tuple-element.198), channel_id=1, source_target_pairs={{0,32},{2,34},{4,36},{6,38},{8,40},{10,42},{12,44},{14,46},{16,48}... | collective-permute-start | bytes 98312 | tf_op jit(solution)/shard_map/ppermute | solution.py:565
  61.6 1.0 %collective-permute-start.16 = (f32[64,128]{1,0:T(8,128)S(1)}, f32[64,128]{1,0:T(8,128)S(1)}, u32[]{:S(2)}, u32[]{:S(2)}) collective-permute-start(f32[64,128]{1,0:T(8,128)S(1)} %get-tuple-element.199), channel_id=1, source_target_pairs={{0,2},{2,0},{4,6},{6,4},{8,10},{10,8},{12,14},{14,12},{16,18},{18,... | collective-permute-start | bytes 98312 | tf_op jit(solution)/shard_map/ppermute | solution.py:568
  62.6 1.5 %collective-permute-start.18 = (f32[64,128]{1,0:T(8,128)S(1)}, f32[64,128]{1,0:T(8,128)S(1)}, u32[]{:S(2)}, u32[]{:S(2)}) collective-permute-start(f32[64,128]{1,0:T(8,128)S(1)} %get-tuple-element.201), channel_id=1, source_target_pairs={{0,32},{2,4},{4,2},{6,8},{8,6},{10,12},{12,10},{14,16},{16,14},{18... | collective-permute-start | bytes 98312 | tf_op jit(solution)/shard_map/ppermute | solution.py:566
  64.1 1.7 %shard_map.83 = (f32[34,144,128]{2,1,0:T(8,128)S(1)}, f32[1,128]{1,0:T(1,128)S(1)}) custom-call(f32[32,128]{1,0:T(8,128)S(1)} %get-tuple-element.203.refs_0_, f32[32,128]{1,0:T(8,128)S(1)} %get-tuple-element.204.refs_1_.refs_6_, f32[32,128]{1,0:T(8,128)S(1)} %get-tuple-element.205.refs_2_, f32[32,128]{1,0:T(8,128)S(1)} %get-tuple-element.206.refs_3_.refs_7_, ...), custom_call_target="tpu_custom_call" | custom-call | flops 30000000 | bytes 1048576 | tf_op jit(solution)/shard_map/pallas_call | solution.py:534
  65.8 0.1 collective-permute-done.18.refs_9_
  65.9 1.5 %shard_map.84 = (f32[32,128]{1,0:T(8,128)S(1)}, f32[32,128]{1,0:T(8,128)S(1)}, f32[128,128]{1,0:T(8,128)S(1)}, f32[32,128]{1,0:T(8,128)S(1)}, f32[32,128]{1,0:T(...) custom-call(f32[64,128]{1,0:T(8,128)S(1)} %get-tuple-element.192.refs_0_, ...), custom_call_target="tpu_custom_call" | custom-call | flops 20000000 | bytes 1048576 | tf_op jit(solution)/shard_map/pallas_call | solution.py:534
  67.4 17.6 %all_to_all.11 = f32[128,1,128]{2,1,0:T(1,128)S(1)} all-to-all(f32[128,1,128]{2,1,0:T(1,128)S(1)} %bitcast.16), channel_id=1, replica_groups=mesh['gx'=4,'gy'=16,'gz'=2] {'gx','gy','gz'}, dimensions={0} | all-to-all | bytes 131072 | tf_op jit(solution)/shard_map/all_to_all | solution.py:574
  85.0 2.2 %shard_map.85 = (f32[32,128,128]{2,1,0:T(8,128)}, f32[32,128]{1,0:T(8,128)}, f32[32,128]{1,0:T(8,128)}, f32[128,128]{1,0:T(8,128)}) custom-call(f32[128,128]{1,0:T(8,128)S(1)} %bitcast.14, f32[34,144,128]{2,1,0:T(8,128)S(1)} %get-tuple-element.211.refs_1_, f32[34,144,128]{2,1,0:T(8,128)S(1)} %get-tuple-element.212.refs_2_, ...), custom_call_target="tpu_custom_call" | custom-call | flops 20000000 | bytes 1048576 | tf_op jit(solution)/shard_map/pallas_call | solution.py:534
  (21 shorter events, 0.1 us)
Async XLA Ops:
  5.2 11.2 %collective-permute-start.4 = (f32[256,128]{1,0:T(8,128)S(1)}, f32[256,128]{1,0:T(8,128)S(1)}, u32[]{:S(2)}, u32[]{:S(2)}) collective-permute-start(f32[256,128]{1,0:T(8,128)S(1)} %get-tuple-element.125), channel_id=1, source_target_pairs={{0,1},{1,0},{2,3},{3,2},{4,5},{5,4},{6,7},{7,6},{8,9},{9,8},{10,11... | collective-permute-start | bytes 393224 | tf_op jit(solution)/shard_map/ppermute | solution.py:567
  8.8 7.5 %collective-permute-start = (f32[160,128]{1,0:T(8,128)S(1)}, f32[160,128]{1,0:T(8,128)S(1)}, u32[]{:S(2)}, u32[]{:S(2)}) collective-permute-start(f32[160,128]{1,0:T(8,128)S(1)} %get-tuple-element.121), channel_id=1, source_target_pairs={{0,32},{2,34},{4,36},{6,38},{8,40},{10,42},{12,44},{14,46},{16,48}... | collective-permute-start | bytes 245768 | tf_op jit(solution)/shard_map/ppermute | solution.py:565
  10.1 6.2 %collective-permute-start.1 = (f32[160,128]{1,0:T(8,128)S(1)}, f32[160,128]{1,0:T(8,128)S(1)}, u32[]{:S(2)}, u32[]{:S(2)}) collective-permute-start(f32[160,128]{1,0:T(8,128)S(1)} %get-tuple-element.122), channel_id=1, source_target_pairs={{0,2},{2,0},{4,6},{6,4},{8,10},{10,8},{12,14},{14,12},{16,18},{18,... | collective-permute-start | bytes 245768 | tf_op jit(solution)/shard_map/ppermute | solution.py:568
  11.4 5.0 %collective-permute-start.2 = (f32[160,128]{1,0:T(8,128)S(1)}, f32[160,128]{1,0:T(8,128)S(1)}, u32[]{:S(2)}, u32[]{:S(2)}) collective-permute-start(f32[160,128]{1,0:T(8,128)S(1)} %get-tuple-element.123), channel_id=1, source_target_pairs={{0,2},{2,0},{4,6},{6,4},{8,10},{10,8},{12,14},{14,12},{16,18},{18,... | collective-permute-start | bytes 245768 | tf_op jit(solution)/shard_map/ppermute | solution.py:569
  11.4 5.0 %collective-permute-start.3 = (f32[160,128]{1,0:T(8,128)S(1)}, f32[160,128]{1,0:T(8,128)S(1)}, u32[]{:S(2)}, u32[]{:S(2)}) collective-permute-start(f32[160,128]{1,0:T(8,128)S(1)} %get-tuple-element.124), channel_id=1, source_target_pairs={{0,32},{2,4},{4,2},{6,8},{8,6},{10,12},{12,10},{14,16},{16,14},{18... | collective-permute-start | bytes 245768 | tf_op jit(solution)/shard_map/ppermute | solution.py:566
  17.6 6.5 %collective-permute-start.9 = (f32[256,128]{1,0:T(8,128)S(1)}, f32[256,128]{1,0:T(8,128)S(1)}, u32[]{:S(2)}, u32[]{:S(2)}) collective-permute-start(f32[256,128]{1,0:T(8,128)S(1)} %get-tuple-element.148), channel_id=1, source_target_pairs={{0,1},{1,0},{2,3},{3,2},{4,5},{5,4},{6,7},{7,6},{8,9},{9,8},{10,11... | collective-permute-start | bytes 393224 | tf_op jit(solution)/shard_map/ppermute | solution.py:567
  17.9 5.8 %collective-permute-start.5 = (f32[64,128]{1,0:T(8,128)S(1)}, f32[64,128]{1,0:T(8,128)S(1)}, u32[]{:S(2)}, u32[]{:S(2)}) collective-permute-start(f32[64,128]{1,0:T(8,128)S(1)} %get-tuple-element.144), channel_id=1, source_target_pairs={{0,32},{2,34},{4,36},{6,38},{8,40},{10,42},{12,44},{14,46},{16,48}... | collective-permute-start | bytes 98312 | tf_op jit(solution)/shard_map/ppermute | solution.py:565
  19.9 3.8 %collective-permute-start.6 = (f32[64,128]{1,0:T(8,128)S(1)}, f32[64,128]{1,0:T(8,128)S(1)}, u32[]{:S(2)}, u32[]{:S(2)}) collective-permute-start(f32[64,128]{1,0:T(8,128)S(1)} %get-tuple-element.145), channel_id=1, source_target_pairs={{0,2},{2,0},{4,6},{6,4},{8,10},{10,8},{12,14},{14,12},{16,18},{18,... | collective-permute-start | bytes 98312 | tf_op jit(solution)/shard_map/ppermute | solution.py:568
  20.4 3.3 %collective-permute-start.7 = (f32[64,128]{1,0:T(8,128)S(1)}, f32[64,128]{1,0:T(8,128)S(1)}, u32[]{:S(2)}, u32[]{:S(2)}) collective-permute-start(f32[64,128]{1,0:T(8,128)S(1)} %get-tuple-element.146), channel_id=1, source_target_pairs={{0,2},{2,0},{4,6},{6,4},{8,10},{10,8},{12,14},{14,12},{16,18},{18,... | collective-permute-start | bytes 98312 | tf_op jit(solution)/shard_map/ppermute | solution.py:569
  20.5 3.6 %collective-permute-start.8 = (f32[64,128]{1,0:T(8,128)S(1)}, f32[64,128]{1,0:T(8,128)S(1)}, u32[]{:S(2)}, u32[]{:S(2)}) collective-permute-start(f32[64,128]{1,0:T(8,128)S(1)} %get-tuple-element.147), channel_id=1, source_target_pairs={{0,32},{2,4},{4,2},{6,8},{8,6},{10,12},{12,10},{14,16},{16,14},{18... | collective-permute-start | bytes 98312 | tf_op jit(solution)/shard_map/ppermute | solution.py:566
  51.0 6.5 %collective-permute-start.14 = (f32[128,128]{1,0:T(8,128)S(1)}, f32[128,128]{1,0:T(8,128)S(1)}, u32[]{:S(2)}, u32[]{:S(2)}) collective-permute-start(f32[128,128]{1,0:T(8,128)S(1)} %get-tuple-element.183), channel_id=1, source_target_pairs={{0,1},{1,0},{2,3},{3,2},{4,5},{5,4},{6,7},{7,6},{8,9},{9,8},{10,11... | collective-permute-start | bytes 196616 | tf_op jit(solution)/shard_map/ppermute | solution.py:567
  52.1 5.3 %collective-permute-start.10 = (f32[32,128]{1,0:T(8,128)S(1)}, f32[32,128]{1,0:T(8,128)S(1)}, u32[]{:S(2)}, u32[]{:S(2)}) collective-permute-start(f32[32,128]{1,0:T(8,128)S(1)} %get-tuple-element.179), channel_id=1, source_target_pairs={{0,32},{2,34},{4,36},{6,38},{8,40},{10,42},{12,44},{14,46},{16,48}... | collective-permute-start | bytes 49160 | tf_op jit(solution)/shard_map/ppermute | solution.py:565
  52.4 5.0 %collective-permute-start.11 = (f32[32,128]{1,0:T(8,128)S(1)}, f32[32,128]{1,0:T(8,128)S(1)}, u32[]{:S(2)}, u32[]{:S(2)}) collective-permute-start(f32[32,128]{1,0:T(8,128)S(1)} %get-tuple-element.180), channel_id=1, source_target_pairs={{0,2},{2,0},{4,6},{6,4},{8,10},{10,8},{12,14},{14,12},{16,18},{18,... | collective-permute-start | bytes 49160 | tf_op jit(solution)/shard_map/ppermute | solution.py:568
  53.5 3.9 %collective-permute-start.12 = (f32[32,128]{1,0:T(8,128)S(1)}, f32[32,128]{1,0:T(8,128)S(1)}, u32[]{:S(2)}, u32[]{:S(2)}) collective-permute-start(f32[32,128]{1,0:T(8,128)S(1)} %get-tuple-element.181), channel_id=1, source_target_pairs={{0,2},{2,0},{4,6},{6,4},{8,10},{10,8},{12,14},{14,12},{16,18},{18,... | collective-permute-start | bytes 49160 | tf_op jit(solution)/shard_map/ppermute | solution.py:569
  53.5 3.9 %collective-permute-start.13 = (f32[32,128]{1,0:T(8,128)S(1)}, f32[32,128]{1,0:T(8,128)S(1)}, u32[]{:S(2)}, u32[]{:S(2)}) collective-permute-start(f32[32,128]{1,0:T(8,128)S(1)} %get-tuple-element.182), channel_id=1, source_target_pairs={{0,32},{2,4},{4,2},{6,8},{8,6},{10,12},{12,10},{14,16},{16,14},{18... | collective-permute-start | bytes 49160 | tf_op jit(solution)/shard_map/ppermute | solution.py:566
  58.6 7.3 %collective-permute-start.19 = (f32[256,128]{1,0:T(8,128)S(1)}, f32[256,128]{1,0:T(8,128)S(1)}, u32[]{:S(2)}, u32[]{:S(2)}) collective-permute-start(f32[256,128]{1,0:T(8,128)S(1)} %get-tuple-element.202), channel_id=1, source_target_pairs={{0,1},{1,0},{2,3},{3,2},{4,5},{5,4},{6,7},{7,6},{8,9},{9,8},{10,11... | collective-permute-start | bytes 393224 | tf_op jit(solution)/shard_map/ppermute | solution.py:567
  60.4 5.4 %collective-permute-start.15 = (f32[64,128]{1,0:T(8,128)S(1)}, f32[64,128]{1,0:T(8,128)S(1)}, u32[]{:S(2)}, u32[]{:S(2)}) collective-permute-start(f32[64,128]{1,0:T(8,128)S(1)} %get-tuple-element.198), channel_id=1, source_target_pairs={{0,32},{2,34},{4,36},{6,38},{8,40},{10,42},{12,44},{14,46},{16,48}... | collective-permute-start | bytes 98312 | tf_op jit(solution)/shard_map/ppermute | solution.py:565
  61.6 4.2 %collective-permute-start.16 = (f32[64,128]{1,0:T(8,128)S(1)}, f32[64,128]{1,0:T(8,128)S(1)}, u32[]{:S(2)}, u32[]{:S(2)}) collective-permute-start(f32[64,128]{1,0:T(8,128)S(1)} %get-tuple-element.199), channel_id=1, source_target_pairs={{0,2},{2,0},{4,6},{6,4},{8,10},{10,8},{12,14},{14,12},{16,18},{18,... | collective-permute-start | bytes 98312 | tf_op jit(solution)/shard_map/ppermute | solution.py:568
  62.6 3.2 %collective-permute-start.17 = (f32[64,128]{1,0:T(8,128)S(1)}, f32[64,128]{1,0:T(8,128)S(1)}, u32[]{:S(2)}, u32[]{:S(2)}) collective-permute-start(f32[64,128]{1,0:T(8,128)S(1)} %get-tuple-element.200), channel_id=1, source_target_pairs={{0,2},{2,0},{4,6},{6,4},{8,10},{10,8},{12,14},{14,12},{16,18},{18,... | collective-permute-start | bytes 98312 | tf_op jit(solution)/shard_map/ppermute | solution.py:569
  62.6 3.3 %collective-permute-start.18 = (f32[64,128]{1,0:T(8,128)S(1)}, f32[64,128]{1,0:T(8,128)S(1)}, u32[]{:S(2)}, u32[]{:S(2)}) collective-permute-start(f32[64,128]{1,0:T(8,128)S(1)} %get-tuple-element.201), channel_id=1, source_target_pairs={{0,32},{2,4},{4,2},{6,8},{8,6},{10,12},{12,10},{14,16},{16,14},{18... | collective-permute-start | bytes 98312 | tf_op jit(solution)/shard_map/ppermute | solution.py:566

commit v3 on v2

--- a/solution.py
+++ b/solution.py
@@ -25,26 +25,22 @@
 PAD = 8
 
 
-def parts_of(a):
-    first = a.astype(BF16)
-    rest = a - first.astype(F32)
-    second = rest.astype(BF16)
-    third = (rest - second.astype(F32)).astype(BF16)
-    return first, second, third
+def parts_of(a, count):
+    parts = []
+    for _ in range(count):
+        parts.append(a.astype(BF16))
+        a = a - parts[-1].astype(F32)
+    return parts
 
 
 def dot(a, parts, d):
     n = a.shape[0]
-    mul = functools.partial(jnp.dot, preferred_element_type=F32)
-    a1, a2, a3 = parts_of(a)
-    r = mul(jnp.concatenate([a1, a2, a3], axis=0), parts[d, :, 0 : 2 * C])
-    t = mul(a1, parts[d, :, 2 * C :])
-    small = r[2 * n :, :C] + r[n : 2 * n, C:] + t
-    return r[:n, :C] + (r[n : 2 * n, :C] + r[:n, C:] + small)
+    r = jnp.dot(jnp.concatenate(parts_of(a, 2), axis=0), parts[d], preferred_element_type=F32)
+    return r[:n, :C] + (r[n:, :C] + r[:n, C:] + r[n:, C:])
 
 
 def store_parts(ref, d, a):
-    for i, p in enumerate(parts_of(a)):
+    for i, p in enumerate(parts_of(a, 2)):
         ref[d, :, i * C : (i + 1) * C] = p
 
 
@@ -290,7 +286,7 @@
         c.wait()
     for d in range(3):
         onehot = jnp.where(row_of((C, C)) == segs[d], 1.0, 0.0).astype(BF16)
-        base = sum(lax.dot_general(onehot, p, (((1,), (1,)), ((), ())), preferred_element_type=F32) for p in reversed(parts_of(proj[d])))
+        base = sum(lax.dot_general(onehot, p, (((1,), (1,)), ((), ())), preferred_element_type=F32) for p in reversed(parts_of(proj[d], 3)))
         store_parts(parts, d, base)
         for a in (sends[:2], sends[2:4])[d] if d < 2 else ():
             a[CZ : CZ + C, :] = base
@@ -520,7 +516,7 @@
 S_SIDE = [pltpu.VMEM(f.shape, F32) for f in SIDE]
 S_FIELD = pltpu.VMEM((CZ, C, C), F32)
 S_PADDED = pltpu.VMEM((CZ + 2, C + 2 * PAD, C), F32)
-PIECES = jax.ShapeDtypeStruct((3, C, 3 * C), BF16)
+PIECES = jax.ShapeDtypeStruct((3, C, 2 * C), BF16)
 S_SQUARE = pltpu.VMEM((C, C), F32)
 
 

time: 87.5 us -> 86.3 us (0.986)
  Pallas kernels: 25.3 us -> 24.2 us
    pallas_call x11, Pallas kernels: 25.3 us -> 24.2 us  [call(): pl.pallas_call(kernel, out_shape=tuple(outs), in_specs=in_specs or [VM] *...]
where the time goes in v3:
time: 86.3 us; the launch traced here: 86.2 us
  blocking collectives  38.9 us (45%)
  Pallas kernels  24.2 us (28%)
  starting transfers between devices  21.6 us (25%)
  between operations  0.96 us (1%)
    all_to_all x2, blocking collectives, gather_rows(): rows = lax.all_to_all(rows.reshape(C, 1, C), AXES, 0, 0)  38.9 us
    pallas_call x11, Pallas kernels, call(): pl.pallas_call(kernel, out_shape=tuple(outs), in_specs=in_specs or [VM] *...  24.2 us
    ppermute x4, starting transfers between devices, exchange(): zz = lax.ppermute(zz, 'gz', [(0, 1), (1, 0)])  6.87 us
    ppermute x4, starting transfers between devices, exchange(): yb = lax.ppermute(yb, both, swap_pairs('y', 1))  5.99 us
    ppermute x4, starting transfers between devices, exchange(): xa = lax.ppermute(xa, both, swap_pairs('x', 0))  4.95 us
    ppermute x4, starting transfers between devices, exchange(): xb = lax.ppermute(xb, both, swap_pairs('x', 1))  3.78 us
  transfers between devices with their start and end apart: 20, of which 2 were waited for; matrix products, arithmetic and copies ran while one was open for 0% of the time, Pallas kernels for 11%

profile of v3, /device:TPU:1, one launch (start us, length us, event | category | flops | bytes accessed | tf_op | source)
XLA Modules:
  0.0 86.2 jit_solution(15151193050908255858)
XLA Ops:
  0.6 4.5 %shard_map.75 = (f32[32,128,128]{2,1,0:T(8,128)S(1)}, f32[34,144,128]{2,1,0:T(8,128)S(1)}, bf16[3,128,256]{2,1,0:T(8,128)(2,1)S(1)}, f32[32,128,128]{2,1,0:T(8,1...) custom-call(f32[32,128,128]{2,1,0:T(8,128)} %heat_in.1, ...), custom_call_target="tpu_custom_call" | custom-call | flops 40000000 | bytes 1048576 | tf_op jit(solution)/shard_map/pallas_call | solution.py:530
  5.2 3.6 %collective-permute-start.4 = (f32[256,128]{1,0:T(8,128)S(1)}, f32[256,128]{1,0:T(8,128)S(1)}, u32[]{:S(2)}, u32[]{:S(2)}) collective-permute-start(f32[256,128]{1,0:T(8,128)S(1)} %get-tuple-element.125), channel_id=1, source_target_pairs={{0,1},{1,0},{2,3},{3,2},{4,5},{5,4},{6,7},{7,6},{8,9},{9,8},{10,11... | collective-permute-start | bytes 393224 | tf_op jit(solution)/shard_map/ppermute | solution.py:563
  8.8 1.3 %collective-permute-start = (f32[160,128]{1,0:T(8,128)S(1)}, f32[160,128]{1,0:T(8,128)S(1)}, u32[]{:S(2)}, u32[]{:S(2)}) collective-permute-start(f32[160,128]{1,0:T(8,128)S(1)} %get-tuple-element.121), channel_id=1, source_target_pairs={{0,32},{2,34},{4,36},{6,38},{8,40},{10,42},{12,44},{14,46},{16,48}... | collective-permute-start | bytes 245768 | tf_op jit(solution)/shard_map/ppermute | solution.py:561
  10.1 1.2 %collective-permute-start.1 = (f32[160,128]{1,0:T(8,128)S(1)}, f32[160,128]{1,0:T(8,128)S(1)}, u32[]{:S(2)}, u32[]{:S(2)}) collective-permute-start(f32[160,128]{1,0:T(8,128)S(1)} %get-tuple-element.122), channel_id=1, source_target_pairs={{0,2},{2,0},{4,6},{6,4},{8,10},{10,8},{12,14},{14,12},{16,18},{18,... | collective-permute-start | bytes 245768 | tf_op jit(solution)/shard_map/ppermute | solution.py:564
  11.3 2.0 %collective-permute-start.3 = (f32[160,128]{1,0:T(8,128)S(1)}, f32[160,128]{1,0:T(8,128)S(1)}, u32[]{:S(2)}, u32[]{:S(2)}) collective-permute-start(f32[160,128]{1,0:T(8,128)S(1)} %get-tuple-element.124), channel_id=1, source_target_pairs={{0,32},{2,4},{4,2},{6,8},{8,6},{10,12},{12,10},{14,16},{16,14},{18... | collective-permute-start | bytes 245768 | tf_op jit(solution)/shard_map/ppermute | solution.py:562
  13.4 2.9 %shard_map.76 = (f32[34,144,128]{2,1,0:T(8,128)S(1)}, f32[32,128]{1,0:T(8,128)S(1)}, f32[32,128]{1,0:T(8,128)S(1)}, f32[32,128]{1,0:T(8,128)S(1)}, f32[32,128]{1...) custom-call(f32[34,144,128]{2,1,0:T(8,128)S(1)} %get-tuple-element.130.state, ...), custom_call_target="tpu_custom_call" | custom-call | flops 30000000 | bytes 1048576 | tf_op jit(solution)/shard_map/pallas_call | solution.py:530
  16.3 1.0 %shard_map.77 = (f32[32,128]{1,0:T(8,128)S(1)}, f32[32,128]{1,0:T(8,128)S(1)}, f32[32,128]{1,0:T(8,128)S(1)}, f32[32,128]{1,0:T(8,128)S(1)}, f32[128,128]{1,0:T(...) custom-call(f32[32,128]{1,0:T(8,128)S(1)} %get-tuple-element.115.ref, ...), custom_call_target="tpu_custom_call" | custom-call | flops 20000000 | bytes 1048576 | tf_op jit(solution)/shard_map/pallas_call | solution.py:530
  17.4 0.3 collective-permute-start.9
  17.7 2.1 %collective-permute-start.5 = (f32[64,128]{1,0:T(8,128)S(1)}, f32[64,128]{1,0:T(8,128)S(1)}, u32[]{:S(2)}, u32[]{:S(2)}) collective-permute-start(f32[64,128]{1,0:T(8,128)S(1)} %get-tuple-element.144), channel_id=1, source_target_pairs={{0,32},{2,34},{4,36},{6,38},{8,40},{10,42},{12,44},{14,46},{16,48}... | collective-permute-start | bytes 98312 | tf_op jit(solution)/shard_map/ppermute | solution.py:561
  19.7 0.5 collective-permute-start.6
  20.2 0.0 collective-permute-start.7
  20.2 1.5 %collective-permute-start.8 = (f32[64,128]{1,0:T(8,128)S(1)}, f32[64,128]{1,0:T(8,128)S(1)}, u32[]{:S(2)}, u32[]{:S(2)}) collective-permute-start(f32[64,128]{1,0:T(8,128)S(1)} %get-tuple-element.147), channel_id=1, source_target_pairs={{0,32},{2,4},{4,2},{6,8},{8,6},{10,12},{12,10},{14,16},{16,14},{18... | collective-permute-start | bytes 98312 | tf_op jit(solution)/shard_map/ppermute | solution.py:562
  21.8 1.7 %shard_map.78 = (f32[34,144,128]{2,1,0:T(8,128)S(1)}, f32[1,128]{1,0:T(1,128)S(1)}) custom-call(f32[32,128]{1,0:T(8,128)S(1)} %get-tuple-element.151.refs_0_.refs_5_, f32[32,128]{1,0:T(8,128)S(1)} %get-tuple-element.152.refs_1_.refs_6_, f32[32,128]{1,0:T(8,128)S(1)} %get-tuple-element.153.refs_2_.refs_7_, f32[32,128]{1,0:T(8,128)S(1)} %get-tuple-element.154.refs_3_.refs_8_, ...), custom_call_target="tpu_custom_call" | custom-call | flops 30000000 | bytes 1048576 | tf_op jit(solution)/shard_map/pallas_call | solution.py:530
  23.5 0.3 collective-permute-done.8.refs_9_
  23.9 1.1 %shard_map.79 = (f32[32,128]{1,0:T(8,128)S(1)}, f32[32,128]{1,0:T(8,128)S(1)}, f32[128,128]{1,0:T(8,128)S(1)}, f32[32,128]{1,0:T(8,128)S(1)}, f32[32,128]{1,0:T(...) custom-call(f32[64,128]{1,0:T(8,128)S(1)} %get-tuple-element.138.ref, ...), custom_call_target="tpu_custom_call" | custom-call | flops 20000000 | bytes 1048576 | tf_op jit(solution)/shard_map/pallas_call | solution.py:530
  25.0 21.4 %all_to_all.10 = f32[128,1,128]{2,1,0:T(1,128)S(1)} all-to-all(f32[128,1,128]{2,1,0:T(1,128)S(1)} %bitcast.15), channel_id=1, replica_groups=mesh['gx'=4,'gy'=16,'gz'=2] {'gx','gy','gz'}, dimensions={0} | all-to-all | bytes 131072 | tf_op jit(solution)/shard_map/all_to_all | solution.py:570
  46.4 4.0 %shard_map.80 = (f32[32,128,128]{2,1,0:T(8,128)S(1)}, f32[34,144,128]{2,1,0:T(8,128)S(1)}, f32[32,128]{1,0:T(8,128)S(1)}, f32[32,128]{1,0:T(8,128)S(1)}, f32[128...) custom-call(f32[128,128]{1,0:T(8,128)S(1)} %bitcast.13, ...), custom_call_target="tpu_custom_call" | custom-call | flops 50000000 | bytes 1048576 | tf_op jit(solution)/shard_map/pallas_call | solution.py:530
  50.4 1.1 %collective-permute-start.14 = (f32[128,128]{1,0:T(8,128)S(1)}, f32[128,128]{1,0:T(8,128)S(1)}, u32[]{:S(2)}, u32[]{:S(2)}) collective-permute-start(f32[128,128]{1,0:T(8,128)S(1)} %get-tuple-element.183), channel_id=1, source_target_pairs={{0,1},{1,0},{2,3},{3,2},{4,5},{5,4},{6,7},{7,6},{8,9},{9,8},{10,11... | collective-permute-start | bytes 196616 | tf_op jit(solution)/shard_map/ppermute | solution.py:563
  51.5 0.4 collective-permute-start.10
  51.9 1.1 %collective-permute-start.11 = (f32[32,128]{1,0:T(8,128)S(1)}, f32[32,128]{1,0:T(8,128)S(1)}, u32[]{:S(2)}, u32[]{:S(2)}) collective-permute-start(f32[32,128]{1,0:T(8,128)S(1)} %get-tuple-element.180), channel_id=1, source_target_pairs={{0,2},{2,0},{4,6},{6,4},{8,10},{10,8},{12,14},{14,12},{16,18},{18,... | collective-permute-start | bytes 49160 | tf_op jit(solution)/shard_map/ppermute | solution.py:564
  53.0 0.9 %collective-permute-start.13 = (f32[32,128]{1,0:T(8,128)S(1)}, f32[32,128]{1,0:T(8,128)S(1)}, u32[]{:S(2)}, u32[]{:S(2)}) collective-permute-start(f32[32,128]{1,0:T(8,128)S(1)} %get-tuple-element.182), channel_id=1, source_target_pairs={{0,32},{2,4},{4,2},{6,8},{8,6},{10,12},{12,10},{14,16},{16,14},{18... | collective-permute-start | bytes 49160 | tf_op jit(solution)/shard_map/ppermute | solution.py:562
  53.9 2.9 %shard_map.81 = (f32[34,144,128]{2,1,0:T(8,128)S(1)}, f32[32,128]{1,0:T(8,128)S(1)}, f32[32,128]{1,0:T(8,128)S(1)}, f32[32,128]{1,0:T(8,128)S(1)}, f32[32,128]{1...) custom-call(f32[34,144,128]{2,1,0:T(8,128)S(1)} %get-tuple-element.184.state, ...), custom_call_target="tpu_custom_call" | custom-call | flops 30000000 | bytes 1048576 | tf_op jit(solution)/shard_map/pallas_call | solution.py:530
  56.9 1.0 %shard_map.82 = (f32[32,128]{1,0:T(8,128)S(1)}, f32[32,128]{1,0:T(8,128)S(1)}, f32[32,128]{1,0:T(8,128)S(1)}, f32[32,128]{1,0:T(8,128)S(1)}, f32[128,128]{1,0:T(...) custom-call(f32[32,128]{1,0:T(8,128)S(1)} %get-tuple-element.173.ref, ...), custom_call_target="tpu_custom_call" | custom-call | flops 20000000 | bytes 1048576 | tf_op jit(solution)/shard_map/pallas_call | solution.py:530
  57.9 1.8 %collective-permute-start.19 = (f32[256,128]{1,0:T(8,128)S(1)}, f32[256,128]{1,0:T(8,128)S(1)}, u32[]{:S(2)}, u32[]{:S(2)}) collective-permute-start(f32[256,128]{1,0:T(8,128)S(1)} %get-tuple-element.202), channel_id=1, source_target_pairs={{0,1},{1,0},{2,3},{3,2},{4,5},{5,4},{6,7},{7,6},{8,9},{9,8},{10,11... | collective-permute-start | bytes 393224 | tf_op jit(solution)/shard_map/ppermute | solution.py:563
  59.6 1.2 %collective-permute-start.15 = (f32[64,128]{1,0:T(8,128)S(1)}, f32[64,128]{1,0:T(8,128)S(1)}, u32[]{:S(2)}, u32[]{:S(2)}) collective-permute-start(f32[64,128]{1,0:T(8,128)S(1)} %get-tuple-element.198), channel_id=1, source_target_pairs={{0,32},{2,34},{4,36},{6,38},{8,40},{10,42},{12,44},{14,46},{16,48}... | collective-permute-start | bytes 98312 | tf_op jit(solution)/shard_map/ppermute | solution.py:561
  60.9 1.0 %collective-permute-start.16 = (f32[64,128]{1,0:T(8,128)S(1)}, f32[64,128]{1,0:T(8,128)S(1)}, u32[]{:S(2)}, u32[]{:S(2)}) collective-permute-start(f32[64,128]{1,0:T(8,128)S(1)} %get-tuple-element.199), channel_id=1, source_target_pairs={{0,2},{2,0},{4,6},{6,4},{8,10},{10,8},{12,14},{14,12},{16,18},{18,... | collective-permute-start | bytes 98312 | tf_op jit(solution)/shard_map/ppermute | solution.py:564
  61.8 1.5 %collective-permute-start.18 = (f32[64,128]{1,0:T(8,128)S(1)}, f32[64,128]{1,0:T(8,128)S(1)}, u32[]{:S(2)}, u32[]{:S(2)}) collective-permute-start(f32[64,128]{1,0:T(8,128)S(1)} %get-tuple-element.201), channel_id=1, source_target_pairs={{0,32},{2,4},{4,2},{6,8},{8,6},{10,12},{12,10},{14,16},{16,14},{18... | collective-permute-start | bytes 98312 | tf_op jit(solution)/shard_map/ppermute | solution.py:562
  63.3 1.7 %shard_map.83 = (f32[34,144,128]{2,1,0:T(8,128)S(1)}, f32[1,128]{1,0:T(1,128)S(1)}) custom-call(f32[32,128]{1,0:T(8,128)S(1)} %get-tuple-element.203.refs_0_, f32[32,128]{1,0:T(8,128)S(1)} %get-tuple-element.204.refs_1_.refs_6_, f32[32,128]{1,0:T(8,128)S(1)} %get-tuple-element.205.refs_2_, f32[32,128]{1,0:T(8,128)S(1)} %get-tuple-element.206.refs_3_.refs_7_, ...), custom_call_target="tpu_custom_call" | custom-call | flops 30000000 | bytes 1048576 | tf_op jit(solution)/shard_map/pallas_call | solution.py:530
  65.1 0.1 collective-permute-done.18.refs_9_
  65.2 1.1 %shard_map.84 = (f32[32,128]{1,0:T(8,128)S(1)}, f32[32,128]{1,0:T(8,128)S(1)}, f32[128,128]{1,0:T(8,128)S(1)}, f32[32,128]{1,0:T(8,128)S(1)}, f32[32,128]{1,0:T(...) custom-call(f32[64,128]{1,0:T(8,128)S(1)} %get-tuple-element.192.refs_0_, ...), custom_call_target="tpu_custom_call" | custom-call | flops 20000000 | bytes 1048576 | tf_op jit(solution)/shard_map/pallas_call | solution.py:530
  66.3 17.6 %all_to_all.11 = f32[128,1,128]{2,1,0:T(1,128)S(1)} all-to-all(f32[128,1,128]{2,1,0:T(1,128)S(1)} %bitcast.16), channel_id=1, replica_groups=mesh['gx'=4,'gy'=16,'gz'=2] {'gx','gy','gz'}, dimensions={0} | all-to-all | bytes 131072 | tf_op jit(solution)/shard_map/all_to_all | solution.py:570
  83.9 2.2 %shard_map.85 = (f32[32,128,128]{2,1,0:T(8,128)}, f32[32,128]{1,0:T(8,128)}, f32[32,128]{1,0:T(8,128)}, f32[128,128]{1,0:T(8,128)}) custom-call(f32[128,128]{1,0:T(8,128)S(1)} %bitcast.14, f32[34,144,128]{2,1,0:T(8,128)S(1)} %get-tuple-element.211.refs_1_, f32[34,144,128]{2,1,0:T(8,128)S(1)} %get-tuple-element.212.refs_2_, ...), custom_call_target="tpu_custom_call" | custom-call | flops 20000000 | bytes 1048576 | tf_op jit(solution)/shard_map/pallas_call | solution.py:530
  (21 shorter events, 0.1 us)
Async XLA Ops:
  5.2 11.2 %collective-permute-start.4 = (f32[256,128]{1,0:T(8,128)S(1)}, f32[256,128]{1,0:T(8,128)S(1)}, u32[]{:S(2)}, u32[]{:S(2)}) collective-permute-start(f32[256,128]{1,0:T(8,128)S(1)} %get-tuple-element.125), channel_id=1, source_target_pairs={{0,1},{1,0},{2,3},{3,2},{4,5},{5,4},{6,7},{7,6},{8,9},{9,8},{10,11... | collective-permute-start | bytes 393224 | tf_op jit(solution)/shard_map/ppermute | solution.py:563
  8.8 7.5 %collective-permute-start = (f32[160,128]{1,0:T(8,128)S(1)}, f32[160,128]{1,0:T(8,128)S(1)}, u32[]{:S(2)}, u32[]{:S(2)}) collective-permute-start(f32[160,128]{1,0:T(8,128)S(1)} %get-tuple-element.121), channel_id=1, source_target_pairs={{0,32},{2,34},{4,36},{6,38},{8,40},{10,42},{12,44},{14,46},{16,48}... | collective-permute-start | bytes 245768 | tf_op jit(solution)/shard_map/ppermute | solution.py:561
  10.1 6.2 %collective-permute-start.1 = (f32[160,128]{1,0:T(8,128)S(1)}, f32[160,128]{1,0:T(8,128)S(1)}, u32[]{:S(2)}, u32[]{:S(2)}) collective-permute-start(f32[160,128]{1,0:T(8,128)S(1)} %get-tuple-element.122), channel_id=1, source_target_pairs={{0,2},{2,0},{4,6},{6,4},{8,10},{10,8},{12,14},{14,12},{16,18},{18,... | collective-permute-start | bytes 245768 | tf_op jit(solution)/shard_map/ppermute | solution.py:564
  11.3 5.0 %collective-permute-start.2 = (f32[160,128]{1,0:T(8,128)S(1)}, f32[160,128]{1,0:T(8,128)S(1)}, u32[]{:S(2)}, u32[]{:S(2)}) collective-permute-start(f32[160,128]{1,0:T(8,128)S(1)} %get-tuple-element.123), channel_id=1, source_target_pairs={{0,2},{2,0},{4,6},{6,4},{8,10},{10,8},{12,14},{14,12},{16,18},{18,... | collective-permute-start | bytes 245768 | tf_op jit(solution)/shard_map/ppermute | solution.py:565
  11.3 5.0 %collective-permute-start.3 = (f32[160,128]{1,0:T(8,128)S(1)}, f32[160,128]{1,0:T(8,128)S(1)}, u32[]{:S(2)}, u32[]{:S(2)}) collective-permute-start(f32[160,128]{1,0:T(8,128)S(1)} %get-tuple-element.124), channel_id=1, source_target_pairs={{0,32},{2,4},{4,2},{6,8},{8,6},{10,12},{12,10},{14,16},{16,14},{18... | collective-permute-start | bytes 245768 | tf_op jit(solution)/shard_map/ppermute | solution.py:562
  17.4 6.5 %collective-permute-start.9 = (f32[256,128]{1,0:T(8,128)S(1)}, f32[256,128]{1,0:T(8,128)S(1)}, u32[]{:S(2)}, u32[]{:S(2)}) collective-permute-start(f32[256,128]{1,0:T(8,128)S(1)} %get-tuple-element.148), channel_id=1, source_target_pairs={{0,1},{1,0},{2,3},{3,2},{4,5},{5,4},{6,7},{7,6},{8,9},{9,8},{10,11... | collective-permute-start | bytes 393224 | tf_op jit(solution)/shard_map/ppermute | solution.py:563
  17.7 5.8 %collective-permute-start.5 = (f32[64,128]{1,0:T(8,128)S(1)}, f32[64,128]{1,0:T(8,128)S(1)}, u32[]{:S(2)}, u32[]{:S(2)}) collective-permute-start(f32[64,128]{1,0:T(8,128)S(1)} %get-tuple-element.144), channel_id=1, source_target_pairs={{0,32},{2,34},{4,36},{6,38},{8,40},{10,42},{12,44},{14,46},{16,48}... | collective-permute-start | bytes 98312 | tf_op jit(solution)/shard_map/ppermute | solution.py:561
  19.7 3.8 %collective-permute-start.6 = (f32[64,128]{1,0:T(8,128)S(1)}, f32[64,128]{1,0:T(8,128)S(1)}, u32[]{:S(2)}, u32[]{:S(2)}) collective-permute-start(f32[64,128]{1,0:T(8,128)S(1)} %get-tuple-element.145), channel_id=1, source_target_pairs={{0,2},{2,0},{4,6},{6,4},{8,10},{10,8},{12,14},{14,12},{16,18},{18,... | collective-permute-start | bytes 98312 | tf_op jit(solution)/shard_map/ppermute | solution.py:564
  20.2 3.3 %collective-permute-start.7 = (f32[64,128]{1,0:T(8,128)S(1)}, f32[64,128]{1,0:T(8,128)S(1)}, u32[]{:S(2)}, u32[]{:S(2)}) collective-permute-start(f32[64,128]{1,0:T(8,128)S(1)} %get-tuple-element.146), channel_id=1, source_target_pairs={{0,2},{2,0},{4,6},{6,4},{8,10},{10,8},{12,14},{14,12},{16,18},{18,... | collective-permute-start | bytes 98312 | tf_op jit(solution)/shard_map/ppermute | solution.py:565
  20.2 3.6 %collective-permute-start.8 = (f32[64,128]{1,0:T(8,128)S(1)}, f32[64,128]{1,0:T(8,128)S(1)}, u32[]{:S(2)}, u32[]{:S(2)}) collective-permute-start(f32[64,128]{1,0:T(8,128)S(1)} %get-tuple-element.147), channel_id=1, source_target_pairs={{0,32},{2,4},{4,2},{6,8},{8,6},{10,12},{12,10},{14,16},{16,14},{18... | collective-permute-start | bytes 98312 | tf_op jit(solution)/shard_map/ppermute | solution.py:562
  50.4 6.5 %collective-permute-start.14 = (f32[128,128]{1,0:T(8,128)S(1)}, f32[128,128]{1,0:T(8,128)S(1)}, u32[]{:S(2)}, u32[]{:S(2)}) collective-permute-start(f32[128,128]{1,0:T(8,128)S(1)} %get-tuple-element.183), channel_id=1, source_target_pairs={{0,1},{1,0},{2,3},{3,2},{4,5},{5,4},{6,7},{7,6},{8,9},{9,8},{10,11... | collective-permute-start | bytes 196616 | tf_op jit(solution)/shard_map/ppermute | solution.py:563
  51.5 5.3 %collective-permute-start.10 = (f32[32,128]{1,0:T(8,128)S(1)}, f32[32,128]{1,0:T(8,128)S(1)}, u32[]{:S(2)}, u32[]{:S(2)}) collective-permute-start(f32[32,128]{1,0:T(8,128)S(1)} %get-tuple-element.179), channel_id=1, source_target_pairs={{0,32},{2,34},{4,36},{6,38},{8,40},{10,42},{12,44},{14,46},{16,48}... | collective-permute-start | bytes 49160 | tf_op jit(solution)/shard_map/ppermute | solution.py:561
  51.9 5.0 %collective-permute-start.11 = (f32[32,128]{1,0:T(8,128)S(1)}, f32[32,128]{1,0:T(8,128)S(1)}, u32[]{:S(2)}, u32[]{:S(2)}) collective-permute-start(f32[32,128]{1,0:T(8,128)S(1)} %get-tuple-element.180), channel_id=1, source_target_pairs={{0,2},{2,0},{4,6},{6,4},{8,10},{10,8},{12,14},{14,12},{16,18},{18,... | collective-permute-start | bytes 49160 | tf_op jit(solution)/shard_map/ppermute | solution.py:564
  53.0 3.9 %collective-permute-start.12 = (f32[32,128]{1,0:T(8,128)S(1)}, f32[32,128]{1,0:T(8,128)S(1)}, u32[]{:S(2)}, u32[]{:S(2)}) collective-permute-start(f32[32,128]{1,0:T(8,128)S(1)} %get-tuple-element.181), channel_id=1, source_target_pairs={{0,2},{2,0},{4,6},{6,4},{8,10},{10,8},{12,14},{14,12},{16,18},{18,... | collective-permute-start | bytes 49160 | tf_op jit(solution)/shard_map/ppermute | solution.py:565
  53.0 3.9 %collective-permute-start.13 = (f32[32,128]{1,0:T(8,128)S(1)}, f32[32,128]{1,0:T(8,128)S(1)}, u32[]{:S(2)}, u32[]{:S(2)}) collective-permute-start(f32[32,128]{1,0:T(8,128)S(1)} %get-tuple-element.182), channel_id=1, source_target_pairs={{0,32},{2,4},{4,2},{6,8},{8,6},{10,12},{12,10},{14,16},{16,14},{18... | collective-permute-start | bytes 49160 | tf_op jit(solution)/shard_map/ppermute | solution.py:562
  57.9 7.3 %collective-permute-start.19 = (f32[256,128]{1,0:T(8,128)S(1)}, f32[256,128]{1,0:T(8,128)S(1)}, u32[]{:S(2)}, u32[]{:S(2)}) collective-permute-start(f32[256,128]{1,0:T(8,128)S(1)} %get-tuple-element.202), channel_id=1, source_target_pairs={{0,1},{1,0},{2,3},{3,2},{4,5},{5,4},{6,7},{7,6},{8,9},{9,8},{10,11... | collective-permute-start | bytes 393224 | tf_op jit(solution)/shard_map/ppermute | solution.py:563
  59.6 5.4 %collective-permute-start.15 = (f32[64,128]{1,0:T(8,128)S(1)}, f32[64,128]{1,0:T(8,128)S(1)}, u32[]{:S(2)}, u32[]{:S(2)}) collective-permute-start(f32[64,128]{1,0:T(8,128)S(1)} %get-tuple-element.198), channel_id=1, source_target_pairs={{0,32},{2,34},{4,36},{6,38},{8,40},{10,42},{12,44},{14,46},{16,48}... | collective-permute-start | bytes 98312 | tf_op jit(solution)/shard_map/ppermute | solution.py:561
  60.9 4.2 %collective-permute-start.16 = (f32[64,128]{1,0:T(8,128)S(1)}, f32[64,128]{1,0:T(8,128)S(1)}, u32[]{:S(2)}, u32[]{:S(2)}) collective-permute-start(f32[64,128]{1,0:T(8,128)S(1)} %get-tuple-element.199), channel_id=1, source_target_pairs={{0,2},{2,0},{4,6},{6,4},{8,10},{10,8},{12,14},{14,12},{16,18},{18,... | collective-permute-start | bytes 98312 | tf_op jit(solution)/shard_map/ppermute | solution.py:564
  61.8 3.2 %collective-permute-start.17 = (f32[64,128]{1,0:T(8,128)S(1)}, f32[64,128]{1,0:T(8,128)S(1)}, u32[]{:S(2)}, u32[]{:S(2)}) collective-permute-start(f32[64,128]{1,0:T(8,128)S(1)} %get-tuple-element.200), channel_id=1, source_target_pairs={{0,2},{2,0},{4,6},{6,4},{8,10},{10,8},{12,14},{14,12},{16,18},{18,... | collective-permute-start | bytes 98312 | tf_op jit(solution)/shard_map/ppermute | solution.py:565
  61.8 3.3 %collective-permute-start.18 = (f32[64,128]{1,0:T(8,128)S(1)}, f32[64,128]{1,0:T(8,128)S(1)}, u32[]{:S(2)}, u32[]{:S(2)}) collective-permute-start(f32[64,128]{1,0:T(8,128)S(1)} %get-tuple-element.201), channel_id=1, source_target_pairs={{0,32},{2,4},{4,2},{6,8},{8,6},{10,12},{12,10},{14,16},{16,14},{18... | collective-permute-start | bytes 98312 | tf_op jit(solution)/shard_map/ppermute | solution.py:562
